TPU v7x, 8 devices: a whole 2x2x1 slice. The times are simulated.
8 devices in a mesh: dp: 2 (over z, y), ep: 4 (over x, core).
Axes of the slice: x: 2, y: 2, z: 1, core: 2. Of those that a mesh axis runs over, the one named last changes fastest.
Arguments:
- x_a: bfloat16 [2048, 2048], P(('dp', 'ep')), parts along dimension 0
- route_a: int32 [2048, 4], P(('dp', 'ep')), parts along dimension 0
- gate_a: float32 [2048, 4], P(('dp', 'ep')), parts along dimension 0
- h_b: bfloat16 [2048, 2048], P(('dp', 'ep')), parts along dimension 0
- attn_b: bfloat16 [2048, 2048], P(('dp', 'ep')), parts along dimension 0
- route_b: int32 [2048, 4], P(('dp', 'ep')), parts along dimension 0
- gate_b: float32 [2048, 4], P(('dp', 'ep')), parts along dimension 0
- w_qkv: bfloat16 [2048, 6144], replicated
- w_o: bfloat16 [2048, 2048], replicated
- w_gate: bfloat16 [60, 2048, 1408], P('ep')
- w_up: bfloat16 [60, 2048, 1408], P('ep')
- w_down: bfloat16 [60, 1408, 2048], P('ep')
Outputs:
- output 1: bfloat16 [2048, 2048], P(('dp', 'ep')), parts along dimension 0
- output 2: bfloat16 [2048, 2048], P(('dp', 'ep')), parts along dimension 0
- output 3: bfloat16 [2048, 6144], P(('dp', 'ep')), parts along dimension 0
There are 2 independent parts. A program takes and returns all parts, laid end to end along the dimension named above; an argument that names none is the same for every part.
All inputs are finite; a program needn't handle non-finite values.
Results may differ from a plain program's by a relative error of at most 0.0114635.
Values are sent between devices in bfloat16 or wider.
A program may use at most 1.25 GiB of HBM per device.

v0:
```python
import jax
import jax.numpy as jnp
from jax import lax
from jax.sharding import PartitionSpec as P


def route_slots(route_ids, n_experts, n_devs, capacity):
    tok_n, top_k = route_ids.shape
    local_n = n_experts // n_devs
    flat_route = route_ids.reshape(tok_n * top_k)
    one_hot = (flat_route[:, None] == jnp.arange(n_experts)[None, :]).astype(jnp.int32)
    slot_rank = jnp.sum((jnp.cumsum(one_hot, axis=0) - 1) * one_hot, axis=1)
    owner = flat_route // local_n
    local_id = flat_route % local_n
    slot_ids = local_id * (n_devs * capacity) + owner * capacity + slot_rank
    return slot_ids.reshape(tok_n, top_k)


def expert_ffn(rows_in, w_gate, w_up, w_down):
    gate_act = jnp.einsum('erd,edf->erf', rows_in, w_gate, preferred_element_type=jnp.float32)
    up_act = jnp.einsum('erd,edf->erf', rows_in, w_up, preferred_element_type=jnp.float32)
    hidden = (jax.nn.silu(gate_act) * up_act).astype(jnp.bfloat16)
    return jnp.einsum('erf,efd->erd', hidden, w_down, preferred_element_type=jnp.float32).astype(jnp.bfloat16)


def moe_local(tokens, route_ids, gate_vals, w_gate, w_up, w_down, n_devs):
    tok_n, model_dim = tokens.shape
    top_k = route_ids.shape[1]
    local_n = w_gate.shape[0]
    n_experts = local_n * n_devs
    capacity = min(tok_n, 2 * ((tok_n * top_k + n_experts - 1) // n_experts))
    n_slots = n_experts * capacity
    slot_ids = route_slots(route_ids, n_experts, n_devs, capacity)
    picker = (slot_ids[:, :, None] == jnp.arange(n_slots)[None, None, :]).astype(jnp.bfloat16)
    placer = jnp.sum(picker, axis=1)
    send_buf = jnp.einsum('ts,td->sd', placer, tokens, preferred_element_type=jnp.float32).astype(jnp.bfloat16)
    send_buf = send_buf.reshape(local_n, n_devs, capacity, model_dim)
    recv_buf = lax.all_to_all(send_buf, 'ep', 1, 1, tiled=True)
    expert_out = expert_ffn(recv_buf.reshape(local_n, n_devs * capacity, model_dim), w_gate, w_up, w_down)
    back_buf = lax.all_to_all(expert_out.reshape(local_n, n_devs, capacity, model_dim), 'ep', 1, 1, tiled=True)
    picked = jnp.einsum('tjs,sd->tjd', picker, back_buf.reshape(n_slots, model_dim), preferred_element_type=jnp.float32)
    mixture = jnp.zeros((tok_n, model_dim), jnp.float32)
    for choice in range(top_k):
        mixture = mixture + gate_vals[:, choice:choice + 1] * picked[:, choice]
    return (tokens.astype(jnp.float32) + mixture).astype(jnp.bfloat16)


def solution(mesh):
    n_devs = mesh.shape['ep']

    def local_step(x_a, route_a, gate_a, h_b, attn_b, route_b, gate_b, w_qkv, w_o, w_gate, w_up, w_down):
        out_a = moe_local(x_a, route_a, gate_a, w_gate, w_up, w_down, n_devs)
        qkv_b = jnp.dot(h_b, w_qkv, preferred_element_type=jnp.float32).astype(jnp.bfloat16)
        proj_b = jnp.dot(attn_b, w_o, preferred_element_type=jnp.float32).astype(jnp.bfloat16)
        mid_b = (h_b.astype(jnp.float32) + proj_b.astype(jnp.float32)).astype(jnp.bfloat16)
        out_b = moe_local(mid_b, route_b, gate_b, w_gate, w_up, w_down, n_devs)
        return out_a, out_b, qkv_b

    row_spec = P(('dp', 'ep'), None)
    full_spec = P(None, None)
    expert_spec = P('ep', None, None)
    return jax.shard_map(
        local_step,
        mesh=mesh,
        in_specs=(row_spec, row_spec, row_spec, row_spec, row_spec, row_spec, row_spec, full_spec, full_spec, expert_spec, expert_spec, expert_spec),
        out_specs=(row_spec, row_spec, row_spec),
        check_vma=False,
    )
```

profile of v0, /device:TPU:0, one launch (start us, length us, event | category | flops | bytes accessed | tf_op | source)
XLA Modules:
  0.0 645.4 jit_solution(8930104534264407967)
XLA Ops:
  1.8 16.9 %reduce-window.16 = s32[60,8,128]{2,1,0:T(8,128)S(1)} reduce-window(s32[60,8,128]{2,1,0:T(8,128)S(1)} %fusion.58, s32[]{:T(128)} %constant.41.clone.1), window={size=1x1x128 pad=0_0x0_0x127_0}, to_apply=%region_4.5 | reduce-window | flops 7802880 | bytes 491524 | tf_op jit(solution)/shard_map/reduce-window.2
  20.9 1.4 fusion.31
  22.4 5.9 fusion.36
  29.3 5.9 convolution_convert_fusion
  35.2 12.4 %reshape.116 = bf16[15,4,36,2048]{3,2,1,0:T(8,128)(2,1)} reshape(bf16[2160,2048]{1,0:T(8,128)(2,1)} %convolution_convert_fusion) | data formatting | bytes 17694720 | tf_op jit(solution)/shard_map/reshape | solution.py:37
  47.6 12.5 %copy.92 = bf16[15,4,36,2048]{3,0,2,1:T(8,128)(2,1)} copy(bf16[15,4,36,2048]{3,2,1,0:T(8,128)(2,1)} %reshape.116) | data formatting | bytes 17694720 | tf_op jit(solution)/shard_map/reshape | solution.py:37
  60.2 6.1 all-to-all-start.2
  66.7 16.9 %reduce-window.14 = s32[60,8,128]{2,1,0:T(8,128)S(1)} reduce-window(s32[60,8,128]{2,1,0:T(8,128)S(1)} %fusion.57, s32[]{:T(128)} %constant.41.clone.1), window={size=1x1x128 pad=0_0x0_0x127_0}, to_apply=%region_0.0 | reduce-window | flops 7802880 | bytes 491524 | tf_op jit(solution)/shard_map/reduce-window
  86.6 5.9 convolution_convert_fusion.1
  92.5 12.5 %reshape.111 = bf16[15,4,36,2048]{3,2,1,0:T(8,128)(2,1)} reshape(bf16[2160,2048]{1,0:T(8,128)(2,1)} %convolution_convert_fusion.1) | data formatting | bytes 17694720 | tf_op jit(solution)/shard_map/reshape | solution.py:37
  105.0 12.5 %copy.82 = bf16[15,4,36,2048]{3,0,2,1:T(8,128)(2,1)} copy(bf16[15,4,36,2048]{3,2,1,0:T(8,128)(2,1)} %reshape.111) | data formatting | bytes 17694720 | tf_op jit(solution)/shard_map/reshape | solution.py:37
  117.5 53.9 %all-to-all-done.2 = bf16[15,4,36,2048]{3,0,2,1:T(8,128)(2,1)} async-done(((bf16[15,4,36,2048]{3,0,2,1:T(8,128)(2,1)}), bf16[15,4,36,2048]{3,0,2,1:T(8,128)(2,1)}, u32[]{:S(2)}, u32[]{:S(2)}) %all-to-all-start.2) | async-done | bytes 8847392 | tf_op jit(solution)/shard_map/all_to_all | solution.py:38
  171.4 6.2 all-to-all-start
  177.6 52.6 %fusion.4 = f32[15,144,1408]{2,1,0:T(8,128)} fusion(bf16[15,2048,1408]{2,1,0:T(8,128)(2,1)} %param.22, bf16[15,144,2048]{2,0,1:T(8,128)(2,1)} %bitcast.15), kind=kOutput, calls=%fused_computation.11 | convolution fusion | flops 12457082880 | bytes 107520000 | tf_op jit(solution)/shard_map/erd,edf->erf/dot_general | solution.py:21
  230.2 54.4 %multiply_convert_fusion.clone.4 = bf16[15,144,1408]{2,1,0:T(8,128)(2,1)} fusion(f32[15,144,1408]{2,1,0:T(8,128)} %fusion.4, bf16[15,2048,1408]{2,1,0:T(8,128)(2,1)} %param.21, bf16[15,144,2048]{2,0,1:T(8,128)(2,1)} %bitcast.15), kind=kOutput, calls=%fused_computation.clone.clone.clone.clone.clone | convolution fusion | flops 12475330560 | bytes 113602560 | tf_op jit(solution)/shard_map/erd,edf->erf/dot_general | solution.py:20
  284.6 34.1 %fusion.27 = bf16[15,144,2048]{2,1,0:T(8,128)(2,1)} fusion(bf16[15,1408,2048]{2,1,0:T(8,128)(2,1)} %param.23, bf16[15,144,1408]{2,1,0:T(8,128)(2,1)} %multiply_convert_fusion.clone.4), kind=kOutput, calls=%fused_computation.24 | convolution fusion | flops 12461506560 | bytes 101437440 | tf_op jit(solution)/shard_map/erf,efd->erd/dot_general | solution.py:23
  318.7 12.2 %copy.95 = bf16[15,144,2048]{2,0,1:T(8,128)(2,1)} copy(bf16[15,144,2048]{2,1,0:T(8,128)(2,1)} %fusion.27) | data formatting | bytes 17694720 | tf_op jit(solution)/shard_map/convert_element_type | solution.py:23
  330.9 6.0 all-to-all-start.3
  337.0 52.6 %fusion.13 = f32[15,144,1408]{2,1,0:T(8,128)} fusion(bf16[15,2048,1408]{2,1,0:T(8,128)(2,1)} %param.22, bf16[15,144,2048]{2,0,1:T(8,128)(2,1)} %bitcast.3), kind=kOutput, calls=%fused_computation.16 | convolution fusion | flops 12457082880 | bytes 107520000 | tf_op jit(solution)/shard_map/erd,edf->erf/dot_general | solution.py:21
  389.5 54.8 %multiply_convert_fusion.1.clone.6 = bf16[15,144,1408]{2,1,0:T(8,128)(2,1)} fusion(f32[15,144,1408]{2,1,0:T(8,128)} %fusion.13, bf16[15,2048,1408]{2,1,0:T(8,128)(2,1)} %param.21, bf16[15,144,2048]{2,0,1:T(8,128)(2,1)} %bitcast.3), kind=kOutput, calls=%fused_computation.1.clone.clone.clone.clone.clone.1 | convolution fusion | flops 12475330560 | bytes 113602560 | tf_op jit(solution)/shard_map/erd,edf->erf/dot_general | solution.py:20
  444.3 34.1 %fusion.24 = bf16[15,144,2048]{2,1,0:T(8,128)(2,1)} fusion(bf16[15,1408,2048]{2,1,0:T(8,128)(2,1)} %param.23, bf16[15,144,1408]{2,1,0:T(8,128)(2,1)} %multiply_convert_fusion.1.clone.6), kind=kOutput, calls=%fused_computation.23 | convolution fusion | flops 12461506560 | bytes 101437440 | tf_op jit(solution)/shard_map/erf,efd->erd/dot_general | solution.py:23
  478.4 12.1 %copy.85 = bf16[15,144,2048]{2,0,1:T(8,128)(2,1)} copy(bf16[15,144,2048]{2,1,0:T(8,128)(2,1)} %fusion.24) | data formatting | bytes 17694720 | tf_op jit(solution)/shard_map/convert_element_type | solution.py:23
  490.5 6.1 all-to-all-start.1
  496.7 12.7 %convolution_convert_fusion.2 = bf16[256,6144]{1,0:T(8,128)(2,1)} fusion(bf16[256,2048]{1,0:T(8,128)(2,1)S(1)} %copy-done.13, bf16[2048,6144]{1,0:T(8,128)(2,1)} %param.19), kind=kOutput, calls=%fused_computation.10 | convolution fusion | flops 6444023808 | bytes 29360128 | tf_op jit(solution)/shard_map/dot_general | solution.py:53
  509.4 12.7 %copy.96 = bf16[15,4,36,2048]{3,2,1,0:T(8,128)(2,1)} copy(bf16[15,4,36,2048]{3,0,2,1:T(8,128)(2,1)} %all-to-all-done.3) | data formatting | bytes 17694720 | tf_op jit(solution)/shard_map/all_to_all | solution.py:40
  522.2 12.5 %reshape.121 = bf16[2160,2048,1]{1,0,2:T(8,128)(2,1)} reshape(bf16[15,4,36,2048]{3,2,1,0:T(8,128)(2,1)} %copy.96) | data formatting | bytes 17694720 | tf_op jit(solution)/shard_map/reshape | solution.py:41
  534.7 14.8 %fusion = f32[256,4,2048]{2,0,1:T(8,128)} fusion(bf16[2160,2048,1]{1,0,2:T(8,128)(2,1)} %reshape.121, s32[256,4]{0,1:T(4,128)S(1)} %copy-done.7), kind=kOutput, calls=%fused_computation.5 | convolution fusion | flops 9061908480 | bytes 17240064 | tf_op jit(solution)/shard_map/tjs,sd->tjd/dot_general | solution.py:41
  549.5 51.2 %all-to-all-done.1 = bf16[15,4,36,2048]{3,0,2,1:T(8,128)(2,1)} async-done(((bf16[15,4,36,2048]{3,0,2,1:T(8,128)(2,1)}), bf16[15,4,36,2048]{3,0,2,1:T(8,128)(2,1)}, u32[]{:S(2)}, u32[]{:S(2)}) %all-to-all-start.1) | async-done | bytes 8847392 | tf_op jit(solution)/shard_map/all_to_all | solution.py:40
  600.7 12.8 %copy.86 = bf16[15,4,36,2048]{3,2,1,0:T(8,128)(2,1)} copy(bf16[15,4,36,2048]{3,0,2,1:T(8,128)(2,1)} %all-to-all-done.1) | data formatting | bytes 17694720 | tf_op jit(solution)/shard_map/all_to_all | solution.py:40
  613.5 12.6 %reshape.120 = bf16[2160,2048,1]{1,0,2:T(8,128)(2,1)} reshape(bf16[15,4,36,2048]{3,2,1,0:T(8,128)(2,1)} %copy.86) | data formatting | bytes 17694720 | tf_op jit(solution)/shard_map/reshape | solution.py:41
  626.1 13.5 %fusion.2 = f32[256,4,2048]{2,0,1:T(8,128)S(1)} fusion(bf16[2160,2048,1]{1,0,2:T(8,128)(2,1)} %reshape.120, s32[256,4]{0,1:T(4,128)S(1)} %copy-done.9), kind=kOutput, calls=%fused_computation.8 | convolution fusion | flops 9061908480 | bytes 17240064 | tf_op jit(solution)/shard_map/tjs,sd->tjd/dot_general | solution.py:41
  639.6 5.3 fusion.40
  (65 shorter events, 7.6 us)
Async XLA Ops:
  0.6 21.7 %copy-start = (bf16[256,2048]{1,0:T(8,128)(2,1)S(1)}, bf16[256,2048]{1,0:T(8,128)(2,1)}, u32[]{:S(2)}) copy-start(bf16[256,2048]{1,0:T(8,128)(2,1)} %param.16) | copy-start | bytes 3145732
  20.3 0.6 copy-start.6
  28.3 1.0 copy-start.4
  60.2 6.2 copy-start.10
  60.2 26.4 %copy-start.2 = (bf16[256,2048]{1,0:T(8,128)(2,1)S(1)}, bf16[256,2048]{1,0:T(8,128)(2,1)}, u32[]{:S(2)}) copy-start(bf16[256,2048]{1,0:T(8,128)(2,1)} %param.12) | copy-start | bytes 3145732
  60.2 111.3 %all-to-all-start.2 = ((bf16[15,4,36,2048]{3,0,2,1:T(8,128)(2,1)}), bf16[15,4,36,2048]{3,0,2,1:T(8,128)(2,1)}, u32[]{:S(2)}, u32[]{:S(2)}) async-start(bf16[15,4,36,2048]{3,0,2,1:T(8,128)(2,1)} %copy.92), calls=%async_computation.2 | async-start | bytes 18874368 | tf_op jit(solution)/shard_map/all_to_all | solution.py:38
  84.6 0.6 copy-start.8
  171.4 159.5 %all-to-all-start = ((bf16[15,4,36,2048]{3,0,2,1:T(8,128)(2,1)}), bf16[15,4,36,2048]{3,0,2,1:T(8,128)(2,1)}, u32[]{:S(2)}, u32[]{:S(2)}) async-start(bf16[15,4,36,2048]{3,0,2,1:T(8,128)(2,1)} %copy.82), calls=%async_computation | async-start | bytes 18874368 | tf_op jit(solution)/shard_map/all_to_all | solution.py:38
  330.9 159.6 %all-to-all-start.3 = ((bf16[15,4,36,2048]{3,0,2,1:T(8,128)(2,1)}), bf16[15,4,36,2048]{3,0,2,1:T(8,128)(2,1)}, u32[]{:S(2)}, u32[]{:S(2)}) async-start(bf16[15,4,36,2048]{3,0,2,1:T(8,128)(2,1)} %bitcast.116), calls=%async_computation.3 | async-start | bytes 18874368 | tf_op jit(solution)/shard_map/all_to_all | solution.py:40
  490.5 6.2 copy-start.11
  490.5 6.2 copy-start.12
  490.5 6.2 copy-start.13
  490.5 110.2 %all-to-all-start.1 = ((bf16[15,4,36,2048]{3,0,2,1:T(8,128)(2,1)}), bf16[15,4,36,2048]{3,0,2,1:T(8,128)(2,1)}, u32[]{:S(2)}, u32[]{:S(2)}) async-start(bf16[15,4,36,2048]{3,0,2,1:T(8,128)(2,1)} %bitcast.115), calls=%async_computation.1 | async-start | bytes 18874368 | tf_op jit(solution)/shard_map/all_to_all | solution.py:40
  522.2 12.5 %copy-start.7 = (s32[256,4]{0,1:T(4,128)S(1)}, s32[256,4]{0,1:T(4,128)}, u32[]{:S(2)}) copy-start(s32[256,4]{0,1:T(4,128)} %copy-done.6) | copy-start | bytes 12292
  613.5 12.6 %copy-start.9 = (s32[256,4]{0,1:T(4,128)S(1)}, s32[256,4]{0,1:T(4,128)}, u32[]{:S(2)}) copy-start(s32[256,4]{0,1:T(4,128)} %copy-done.8) | copy-start | bytes 12292
  626.1 13.5 %copy-start.3 = (bf16[256,2048]{1,0:T(8,128)(2,1)S(1)}, bf16[256,2048]{1,0:T(8,128)(2,1)}, u32[]{:S(2)}) copy-start(bf16[256,2048]{1,0:T(8,128)(2,1)} %param.12) | copy-start | bytes 3145732
  626.1 13.5 %copy-start.5 = (bf16[256,2048]{1,0:T(8,128)(2,1)S(1)}, bf16[256,2048]{1,0:T(8,128)(2,1)}, u32[]{:S(2)}) copy-start(bf16[256,2048]{1,0:T(8,128)(2,1)} %copy-done.4) | copy-start | bytes 3145732
  639.6 5.4 copy-start.1
where the time goes:
time: 656 us; the launch traced here: 645 us
  matrix products  341 us (52%)
  local copies, waits for them, and re-layouts  130 us (20%)
  waiting for transfers between devices  105 us (16%)
  other arithmetic  43.1 us (7%)
  starting transfers between devices  24.5 us (4%)
    dot_general x2, matrix products, expert_ffn(): jnp.einsum('erd,edf->erf', rows_in, w_gate, preferred_element_type=jnp.fl...  109 us
    dot_general x2, matrix products, expert_ffn(): jnp.einsum('erd,edf->erf', rows_in, w_up, preferred_element_type=jnp.floa...  105 us
    dot_general x2, matrix products, expert_ffn(): jnp.einsum('erf,efd->erd', hidden, w_down, preferred_element_type=jnp.flo...  68.2 us
    all_to_all x2, waiting for transfers between devices, moe_local(): recv_buf = lax.all_to_all(send_buf, 'ep', 1, 1, tiled=True)  53.9 us
    all_to_all x2, waiting for transfers between devices, moe_local(): lax.all_to_all(expert_out.reshape(local_n, n_devs, capacity, model_dim),...  51.2 us
    reshape x4, local copies, waits for them, and re-layouts, moe_local(): send_buf = send_buf.reshape(local_n, n_devs, capacity, model_dim)  50 us
    another operation x4, other arithmetic  33.8 us
    dot_general x2, matrix products, moe_local(): jnp.einsum('tjs,sd->tjd', picker, back_buf.reshape(n_slots, model_dim), p...  28.3 us
  transfers between devices with their start and end apart: 4, of which 2 were waited for; matrix products, arithmetic and copies ran while one was open for 64% of the time, Pallas kernels for 0%

commit v1 on v0

v1 whole, which is shorter than its diff:
```python
import functools

import jax
import jax.numpy as jnp
from jax import lax
from jax.experimental import pallas as pl
from jax.experimental.pallas import tpu as pltpu
from jax.sharding import PartitionSpec as P


WIN = 48
STRIDE = 32
SLOTS = 144
F32 = jnp.float32
BF16 = jnp.bfloat16
VMEM_LIMIT = 60 * 1024 * 1024


def permute(x, bit, n):
    return lax.ppermute(x, 'ep', [(i, i ^ bit) for i in range(n)])


def spread(x, n):
    peer = permute(x, 2, n)
    sib = permute(x, 1, n)
    return (x, sib, peer, permute(peer, 1, n))


def routing_tables(route_ids, gate_vals, local_n, me):
    n_src, tok_n, _ = route_ids.shape
    local = route_ids - me * local_n
    experts = jnp.arange(16)
    hit = (local[..., None] == experts) & (experts < local_n)
    chosen = jnp.any(hit, axis=2)
    gates = jnp.sum(jnp.where(hit, gate_vals[..., None], 0.0), axis=2)
    lower = (jnp.arange(tok_n)[:, None] > jnp.arange(tok_n)[None, :]).astype(BF16)
    rank = jnp.einsum('ut,ste->sue', lower, chosen.astype(BF16), preferred_element_type=F32)
    shift = 4.0 * jnp.arange(n_src, dtype=F32)[:, None, None]
    place = jnp.where(chosen, rank + shift, -1.0)
    return place, gates


def gate_up_kernel(n_mb, e0, ne, *refs):
    x_refs = refs[:4 * n_mb]
    place_refs = refs[4 * n_mb:5 * n_mb]
    wg_ref, wu_ref, h_ref, xs_ref = refs[5 * n_mb:]
    step = pl.program_id(0)
    dim = xs_ref.shape[2]
    ff = wg_ref.shape[2]

    @pl.when(step == 0)
    def _():
        for m in range(n_mb):
            for k in range(4):
                tok_n = x_refs[0].shape[0]
                rows = lax.broadcasted_iota(jnp.int32, (WIN, tok_n), 0).astype(F32)
                picks = [
                    jnp.where(jnp.broadcast_to(place_refs[m][k, e0 + e:e0 + e + 1, :], (WIN, tok_n)) == rows, 1.0, 0.0).astype(BF16)
                    for e in range(ne)
                ]
                pick = jnp.concatenate(picks, axis=0)
                lo = SLOTS * m + STRIDE * k

                def column(c, carry):
                    cols = pl.ds(pl.multiple_of(c * 512, 512), 512)
                    rows_in = jnp.dot(pick, x_refs[4 * m + k][:, cols], preferred_element_type=F32)
                    rows_in = rows_in.astype(BF16).reshape(ne, WIN, 512)
                    if k == 0:
                        xs_ref[:, lo:lo + WIN, cols] = rows_in
                    else:
                        xs_ref[:, lo:lo + 16, cols] += rows_in[:, :16]
                        xs_ref[:, lo + 16:lo + WIN, cols] = rows_in[:, 16:]
                    return carry

                lax.fori_loop(0, dim // 512, column, 0)

    x = xs_ref[step]
    full = (ff // 256) * 256
    for c in range(0, full, 256):
        g = jnp.dot(x, wg_ref[0, :, c:c + 256], preferred_element_type=F32)
        u = jnp.dot(x, wu_ref[0, :, c:c + 256], preferred_element_type=F32)
        h_ref[0, :, c:c + 256] = (jax.nn.silu(g) * u).astype(BF16)
    if full < ff:
        both = jnp.concatenate([wg_ref[0, :, full:], wu_ref[0, :, full:]], axis=1)
        gu = jnp.dot(x, both, preferred_element_type=F32)
        g = gu[:, :ff - full]
        u = gu[:, ff - full:]
        h_ref[0, :, full:] = (jax.nn.silu(g) * u).astype(BF16)


def gate_up(xs, places, w_gate, w_up, e0, ne):
    n_mb = len(xs)
    tok_n, dim = xs[0][0].shape
    ff = w_gate.shape[2]
    rows = n_mb * SLOTS
    whole2 = pl.BlockSpec((tok_n, dim), lambda i: (0, 0), pipeline_mode=pl.Buffered(1))
    whole3 = pl.BlockSpec(places[0].shape, lambda i: (0, 0, 0), pipeline_mode=pl.Buffered(1))
    return pl.pallas_call(
        functools.partial(gate_up_kernel, n_mb, e0, ne),
        grid=(ne,),
        in_specs=[whole2] * (4 * n_mb) + [whole3] * n_mb + [
            pl.BlockSpec((1, dim, ff), lambda i: (e0 + i, 0, 0)),
            pl.BlockSpec((1, dim, ff), lambda i: (e0 + i, 0, 0)),
        ],
        out_specs=pl.BlockSpec((1, rows, ff), lambda i: (i, 0, 0)),
        out_shape=jax.ShapeDtypeStruct((ne, rows, ff), BF16),
        scratch_shapes=[pltpu.VMEM((ne, rows, dim), BF16)],
        compiler_params=pltpu.CompilerParams(vmem_limit_bytes=VMEM_LIMIT, dimension_semantics=('arbitrary',)),
        cost_estimate=pl.CostEstimate(
            flops=ne * 4 * 288 * dim * ff, bytes_accessed=ne * 4 * dim * ff, transcendentals=ne * rows * ff),
    )(*[x for group in xs for x in group], *places, w_gate, w_up)


def mix_tables(place, gates):
    hi = gates.astype(BF16)
    rest = gates - hi.astype(F32)
    mid = rest.astype(BF16)
    low = (rest - mid.astype(F32)).astype(BF16)
    return jnp.concatenate([place.astype(BF16), hi, mid, low], axis=2)


def down_kernel(n_exp, groups, part_rows, *refs):
    h_refs = refs[:len(part_rows)]
    w_ref, mix_ref, z_ref, y_ref, g_ref = refs[len(part_rows):]
    j, q = pl.program_id(0), pl.program_id(1)
    per = n_exp // groups
    width = w_ref.shape[2]

    @pl.when((j == 0) & (q == 0))
    def _():
        lanes = g_ref.shape[3]
        col = lax.broadcasted_iota(jnp.int32, (16, lanes), 1)
        first = WIN * lax.broadcasted_iota(jnp.int32, (16, lanes), 0)
        expand = jnp.where((col >= first) & (col < first + WIN), 1.0, 0.0).astype(BF16)
        offset = jnp.sum(jnp.where((col >= first) & (col < first + WIN), (col - first).astype(F32), 0.0), axis=0, keepdims=True)
        for k in range(4):
            mixed = mix_ref[k]
            place = jnp.dot(mixed[:, :16], expand, preferred_element_type=F32)
            here = place == offset
            for i in range(3):
                part = jnp.dot(mixed[:, 16 * i + 16:16 * i + 32], expand, preferred_element_type=F32)
                g_ref[k, i] = jnp.where(here, part, 0.0).astype(BF16)

    for gi in range(groups):
        @pl.when(q == gi)
        def _():
            for e in range(per):
                expert = gi * per + e
                lo = 0
                for part, (count, first) in enumerate(part_rows):
                    if lo <= expert < lo + count:
                        h = h_refs[part][expert - lo, first:first + SLOTS, :]
                    lo += count
                y = jnp.dot(h, w_ref[e], preferred_element_type=F32)
                y_ref[expert] = y.astype(BF16)

    @pl.when(q == groups - 1)
    def _():
        for k in range(4):
            y = y_ref[:, STRIDE * k:STRIDE * k + WIN, :].reshape(n_exp * WIN, width)
            z = jnp.dot(g_ref[k, 0], y, preferred_element_type=F32)
            z = z + jnp.dot(g_ref[k, 1], y, preferred_element_type=F32)
            z = z + jnp.dot(g_ref[k, 2], y, preferred_element_type=F32)
            z_ref[k] = z


def down_mix(hs, part_rows, w_down, mixed, c0, nc, width):
    n_exp, ff, _ = w_down.shape
    tok_n = mixed.shape[1]
    groups = 3
    per = n_exp // groups

    def whole(a):
        zeros = (0,) * a.ndim
        return pl.BlockSpec(a.shape, lambda j, q: zeros, pipeline_mode=pl.Buffered(1))

    return pl.pallas_call(
        functools.partial(down_kernel, n_exp, groups, part_rows),
        grid=(nc, groups),
        in_specs=[whole(h) for h in hs] + [
            pl.BlockSpec((per, ff, width), lambda j, q: (q, 0, c0 + j)),
            whole(mixed),
        ],
        out_specs=pl.BlockSpec((4, tok_n, width), lambda j, q: (0, 0, j)),
        out_shape=jax.ShapeDtypeStruct((4, tok_n, nc * width), F32),
        scratch_shapes=[
            pltpu.VMEM((n_exp, SLOTS, width), BF16),
            pltpu.VMEM((4, 3, tok_n, n_exp * WIN), BF16),
        ],
        compiler_params=pltpu.CompilerParams(vmem_limit_bytes=VMEM_LIMIT, dimension_semantics=('arbitrary', 'arbitrary')),
        cost_estimate=pl.CostEstimate(
            flops=nc * width * n_exp * 8 * 288 * ff, bytes_accessed=nc * width * n_exp * 2 * ff, transcendentals=0),
    )(*hs, w_down, mixed)


def solution(mesh):
    n = mesh.shape['ep']

    def layer(x_a, route_a, gate_a, h_b, attn_b, route_b, gate_b, w_qkv, w_o, w_gate, w_up, w_down):
        me = lax.axis_index('ep')
        local_n = w_gate.shape[0]
        dim = x_a.shape[1]
        small = jnp.concatenate([route_a.astype(F32), route_b.astype(F32), gate_a, gate_b], axis=1)
        small = jnp.stack(spread(small, n))
        xs_a = spread(x_a, n)
        routes = small[..., :8].astype(jnp.int32)
        place_a, gates_a = routing_tables(routes[..., :4], small[..., 8:12], local_n, me)
        place_b, gates_b = routing_tables(routes[..., 4:], small[..., 12:], local_n, me)
        mixed_a, mixed_b = mix_tables(place_a, gates_a), mix_tables(place_b, gates_b)
        place_a, place_b = place_a.transpose(0, 2, 1), place_b.transpose(0, 2, 1)

        proj_b = jnp.dot(attn_b, w_o, preferred_element_type=F32).astype(BF16)
        u_b = (h_b.astype(F32) + proj_b.astype(F32)).astype(BF16)
        xs_b = spread(u_b, n)
        qkv_b = jnp.dot(h_b, w_qkv, preferred_element_type=F32).astype(BF16)

        split = 7
        width, per_call = 512, 2
        h_a1 = gate_up((xs_a,), (place_a,), w_gate, w_up, 0, split)
        h_ab = gate_up((xs_a, xs_b), (place_a, place_b), w_gate, w_up, split, local_n - split)

        def combine(u, hs, first, mixed):
            outs = []
            parts = ((split, 0), (local_n - split, first))
            for c in range(0, dim // width, per_call):
                z = down_mix(hs, parts, w_down, mixed, c, per_call, width)
                got = permute(z[1::2], 1, n)
                mine = z[0] + got[0]
                there = z[2] + got[1]
                back = permute(there, 2, n)
                lo = c * width
                cols = u[:, lo:lo + per_call * width].astype(F32)
                outs.append((cols + (mine + back)).astype(BF16))
            return jnp.concatenate(outs, axis=1)

        out_a = combine(x_a, (h_a1, h_ab), 0, mixed_a)
        h_b1 = gate_up((xs_b,), (place_b,), w_gate, w_up, 0, split)
        out_b = combine(u_b, (h_b1, h_ab), SLOTS, mixed_b)
        return out_a, out_b, qkv_b

    row_spec = P(('dp', 'ep'), None)
    full_spec = P(None, None)
    expert_spec = P('ep', None, None)
    return jax.shard_map(
        layer,
        mesh=mesh,
        in_specs=(row_spec, row_spec, row_spec, row_spec, row_spec, row_spec, row_spec, full_spec, full_spec, expert_spec, expert_spec, expert_spec),
        out_specs=(row_spec, row_spec, row_spec),
        check_vma=False,
    )
```

time: 656 us -> 397 us (0.61)
  matrix products: 341 us -> 21.1 us
  Pallas kernels: 0 us -> 222 us
  local copies, waits for them, and re-layouts: 130 us -> 24 us
  other arithmetic: 43.1 us -> 24 us
  waiting for transfers between devices: 105 us -> 88.1 us
  starting transfers between devices: 24.5 us -> 11.6 us
    dot_general x12 -> x4, matrix products: 341 us -> 21.1 us  [the longest x1 13 us: layer(): qkv_b = jnp.dot(h_b, w_qkv, preferred_element_type=F32).astype(BF16)]
    pallas_call x0 -> x7, Pallas kernels: none -> 222 us  [the longest x3 114 us: gate_up(): pl.pallas_call(functools.partial(gate_up_kernel, n_mb, e0, ne), grid=(ne,...]
    all_to_all x4 -> x0, waiting for transfers between devices: 105 us -> none  [the longest x2 53.9 us: moe_local(): recv_buf = lax.all_to_all(send_buf, 'ep', 1, 1, tiled=True)]
    ppermute x0 -> x17, waiting for transfers between devices: none -> 88.1 us  [permute(): return lax.ppermute(x, 'ep', [(i, i ^ bit) for i in range(n)])]
    reshape x6 -> x0, local copies, waits for them, and re-layouts: 75.1 us -> none  [the longest x4 50 us: moe_local(): send_buf = send_buf.reshape(local_n, n_devs, capacity, model_dim)]
    another operation x4 -> x2, other arithmetic: 33.8 us -> 0.72 us  [layer(): small = jnp.stack(spread(small, n))]
    all_to_all x2 -> x0, local copies, waits for them, and re-layouts: 25.6 us -> none  [moe_local(): lax.all_to_all(expert_out.reshape(local_n, n_devs, capacity, model_dim),...]
    all_to_all x4 -> x0, starting transfers between devices: 24.5 us -> none  [the longest x2 12.3 us: moe_local(): recv_buf = lax.all_to_all(send_buf, 'ep', 1, 1, tiled=True)]
  transfers between devices with their start and end apart: 4 -> 17, of which waited for: 2 -> 6; matrix products, arithmetic and copies ran while one was open for 64% -> 15% of each run, Pallas kernels for 0% -> 31%
where the time goes in v1:
time: 397 us; the launch traced here: 392 us
  Pallas kernels  222 us (56%)
  waiting for transfers between devices  88.1 us (22%)
  local copies, waits for them, and re-layouts  24 us (6%)
  other arithmetic  24 us (6%)
  matrix products  21.1 us (5%)
  starting transfers between devices  11.6 us (3%)
    pallas_call x3, Pallas kernels, gate_up(): pl.pallas_call(functools.partial(gate_up_kernel, n_mb, e0, ne), grid=(ne,...  114 us
    pallas_call x4, Pallas kernels, down_mix(): pl.pallas_call(functools.partial(down_kernel, n_exp, groups, part_rows),...  108 us
    ppermute x17, waiting for transfers between devices, permute(): return lax.ppermute(x, 'ep', [(i, i ^ bit) for i in range(n)])  88.1 us
    dot_general x1, matrix products, layer(): qkv_b = jnp.dot(h_b, w_qkv, preferred_element_type=F32).astype(BF16)  13 us
    ppermute x17, starting transfers between devices, permute(): return lax.ppermute(x, 'ep', [(i, i ^ bit) for i in range(n)])  11.6 us
    slice x4, local copies, waits for them, and re-layouts, combine(): got = permute(z[1::2], 1, n)  8.46 us
  transfers between devices with their start and end apart: 17, of which 6 were waited for; matrix products, arithmetic and copies ran while one was open for 15% of the time, Pallas kernels for 31%

profile of v1, /device:TPU:0, one launch (start us, length us, event | category | flops | bytes accessed | tf_op | source)
XLA Modules:
  0.0 391.9 jit_solution(8796637245504105517)
XLA Ops:
  2.8 3.3 collective-permute-start.4
  6.2 5.9 %fusion.2.refs_4_.refs_0_ = bf16[256,2048]{1,0:T(8,128)(2,1)S(1)} fusion(bf16[256,2048]{1,0:T(8,128)(2,1)S(1)} %copy-done, bf16[2048,2048]{1,0:T(8,128)(2,1)} %param.20, bf16[256,2048]{1,0:T(8,128)(2,1)} %param.15), kind=kOutput, calls=%fused_computation.4 | convolution fusion | flops 2150105088 | bytes 11534336 | tf_op jit(solution)/shard_map/dot_general | solution.py:212
  12.7 1.7 collective-permute-start.1
  19.1 19.2 %collective-permute-done.7.refs_6_.refs_2_ = bf16[256,2048]{1,0:T(8,128)(2,1)} collective-permute-done((bf16[256,2048]{1,0:T(8,128)(2,1)S(1)}, bf16[256,2048]{1,0:T(8,128)(2,1)}, u32[]{:S(2)}, u32[]{:S(2)}) %collective-permute-start.7) | collective-permute-done | bytes 1048608 | tf_op jit(solution)/shard_map/ppermute | solution.py:20
  40.3 1.9 copy.54
  42.1 1.7 copy.55
  46.9 1.9 copy.49
  48.7 1.7 copy.50
  52.0 1.8 copy.43.refs_4_.refs_8_
  53.9 1.8 copy.47.refs_9_.refs_4_
  57.1 2.1 pad_maximum_fusion.3.refs_3_
  61.0 33.2 %shard_map.143.refs_0_ = bf16[7,144,1408]{2,1,0:T(8,128)(2,1)} custom-call(bf16[256,2048]{1,0:T(8,128)(2,1)} %copy-done.4, bf16[256,2048]{1,0:T(8,128)(2,1)} %collective-permute-done.6.refs_5_.refs_1_, bf16[256,2048]{1,0:T(8,128)(2,1)} %collective-permute-done.7.refs_6_.refs_2_, bf16[256,2048]{1,0:T(8,128)(2,1)} %collective-permute-done.8.refs_7_.refs_3_, ...), custom_call_target="tpu_custom_call" | custom-call | flops 23253221376 | bytes 80740352 | tf_op jit(solution)/shard_map/pallas_call | solution.py:98
  94.2 48.4 %shard_map.140.refs_1_ = bf16[8,288,1408]{2,1,0:T(8,128)(2,1)} custom-call(bf16[256,2048]{1,0:T(8,128)(2,1)} %refs_0_.3, bf16[256,2048]{1,0:T(8,128)(2,1)} %collective-permute-done.refs_1_, bf16[256,2048]{1,0:T(8,128)(2,1)} %copy-done.6, bf16[256,2048]{1,0:T(8,128)(2,1)} %collective-permute-done.2.refs_3_, bf16[256,2048]{1,0:T(8,128)(2,1)} %copy-done.4, ...), custom_call_target="tpu_custom_call" | custom-call | flops 26575110144 | bytes 92274688 | tf_op jit(solution)/shard_map/pallas_call | solution.py:98
  142.6 26.8 %shard_map.145 = f32[4,256,1024]{2,1,0:T(8,128)} custom-call(bf16[7,144,1408]{2,1,0:T(8,128)(2,1)} %shard_map.143.refs_0_, bf16[8,288,1408]{2,1,0:T(8,128)(2,1)} %shard_map.140.refs_1_, bf16[15,1408,2048]{2,1,0:T(8,128)(2,1)} %refs_2_.7, bf16[4,256,64]{2,1,0:T(8,128)(2,1)} %pad_maximum_fusion.3.refs_3_), custom_call_target="tpu_custom_call" | custom-call | flops 49828331520 | bytes 43253760 | tf_op jit(solution)/shard_map/pallas_call | solution.py:177
  169.4 27.1 %shard_map.144 = f32[4,256,1024]{2,1,0:T(8,128)} custom-call(bf16[7,144,1408]{2,1,0:T(8,128)(2,1)} %shard_map.143.refs_0_, bf16[8,288,1408]{2,1,0:T(8,128)(2,1)} %shard_map.140.refs_1_, bf16[15,1408,2048]{2,1,0:T(8,128)(2,1)} %refs_2_.7, bf16[4,256,64]{2,1,0:T(8,128)(2,1)} %pad_maximum_fusion.3.refs_3_), custom_call_target="tpu_custom_call" | custom-call | flops 49828331520 | bytes 43253760 | tf_op jit(solution)/shard_map/pallas_call | solution.py:177
  196.5 3.3 slice.112
  201.8 32.7 %shard_map.139.refs_0_ = bf16[7,144,1408]{2,1,0:T(8,128)(2,1)} custom-call(bf16[256,2048]{1,0:T(8,128)(2,1)} %refs_0_.3, bf16[256,2048]{1,0:T(8,128)(2,1)} %collective-permute-done.refs_1_, bf16[256,2048]{1,0:T(8,128)(2,1)} %copy-done.6, bf16[256,2048]{1,0:T(8,128)(2,1)} %collective-permute-done.2.refs_3_, f32[4,16,256]{2,1,0:T(8,128)} %copy.43.refs_4_.refs_8_, ...), custom_call_target="tpu_custom_call" | custom-call | flops 23253221376 | bytes 80740352 | tf_op jit(solution)/shard_map/pallas_call | solution.py:98
  234.5 26.9 %shard_map.142 = f32[4,256,1024]{2,1,0:T(8,128)} custom-call(bf16[7,144,1408]{2,1,0:T(8,128)(2,1)} %shard_map.139.refs_0_, bf16[8,288,1408]{2,1,0:T(8,128)(2,1)} %shard_map.140.refs_1_, bf16[15,1408,2048]{2,1,0:T(8,128)(2,1)} %refs_2_.7, bf16[4,256,64]{2,1,0:T(8,128)(2,1)} %pad_maximum_fusion.2.refs_3_), custom_call_target="tpu_custom_call" | custom-call | flops 49828331520 | bytes 43253760 | tf_op jit(solution)/shard_map/pallas_call | solution.py:177
  261.3 1.8 slice.99
  263.2 27.0 %shard_map.141 = f32[4,256,1024]{2,1,0:T(8,128)} custom-call(bf16[7,144,1408]{2,1,0:T(8,128)(2,1)} %shard_map.139.refs_0_, bf16[8,288,1408]{2,1,0:T(8,128)(2,1)} %shard_map.140.refs_1_, bf16[15,1408,2048]{2,1,0:T(8,128)(2,1)} %refs_2_.7, bf16[4,256,64]{2,1,0:T(8,128)(2,1)} %pad_maximum_fusion.2.refs_3_), custom_call_target="tpu_custom_call" | custom-call | flops 49828331520 | bytes 43253760 | tf_op jit(solution)/shard_map/pallas_call | solution.py:177
  290.2 1.9 slice.93
  293.1 1.6 fusion.3
  294.8 1.8 fusion.8
  296.6 1.9 collective-permute-start.14
  300.3 1.9 collective-permute-start.10
  302.1 13.0 %convolution_convert_fusion = bf16[256,6144]{1,0:T(8,128)(2,1)} fusion(bf16[256,2048]{1,0:T(8,128)(2,1)} %param.15, bf16[2048,6144]{1,0:T(8,128)(2,1)} %param.19), kind=kOutput, calls=%fused_computation | convolution fusion | flops 6444023808 | bytes 29360128 | tf_op jit(solution)/shard_map/dot_general | solution.py:215
  315.1 5.7 %collective-permute-done.16 = f32[256,1024]{1,0:T(8,128)} collective-permute-done((f32[256,1024]{1,0:T(8,128)S(1)}, f32[256,1024]{1,0:T(8,128)}, u32[]{:S(2)}, u32[]{:S(2)}) %collective-permute-start.16) | collective-permute-done | bytes 1048608 | tf_op jit(solution)/shard_map/ppermute | solution.py:20
  320.9 22.5 %collective-permute-done.14 = f32[256,1024]{1,0:T(8,128)} collective-permute-done((f32[256,1024]{1,0:T(8,128)S(1)}, f32[256,1024]{1,0:T(8,128)}, u32[]{:S(2)}, u32[]{:S(2)}) %collective-permute-start.14) | collective-permute-done | bytes 1048608 | tf_op jit(solution)/shard_map/ppermute | solution.py:20
  343.4 3.3 fusion.12
  347.7 18.1 %collective-permute-done.12 = f32[256,1024]{1,0:T(8,128)} collective-permute-done((f32[256,1024]{1,0:T(8,128)S(1)}, f32[256,1024]{1,0:T(8,128)}, u32[]{:S(2)}, u32[]{:S(2)}) %collective-permute-start.12) | collective-permute-done | bytes 1048608 | tf_op jit(solution)/shard_map/ppermute | solution.py:20
  365.8 22.0 %collective-permute-done.10 = f32[256,1024]{1,0:T(8,128)} collective-permute-done((f32[256,1024]{1,0:T(8,128)S(1)}, f32[256,1024]{1,0:T(8,128)}, u32[]{:S(2)}, u32[]{:S(2)}) %collective-permute-start.10) | collective-permute-done | bytes 1048608 | tf_op jit(solution)/shard_map/ppermute | solution.py:20
  387.8 2.8 fusion.22
  (84 shorter events, 24.0 us)
Async XLA Ops:
  0.6 5.5 %copy-start = (bf16[256,2048]{1,0:T(8,128)(2,1)S(1)}, bf16[256,2048]{1,0:T(8,128)(2,1)}, u32[]{:S(2)}) copy-start(bf16[256,2048]{1,0:T(8,128)(2,1)} %param.16) | copy-start | bytes 3145732
  2.8 9.9 %copy-start.2 = (bf16[256,2048]{1,0:T(8,128)(2,1)S(1)}, bf16[256,2048]{1,0:T(8,128)(2,1)}, u32[]{:S(2)}) copy-start(bf16[256,2048]{1,0:T(8,128)(2,1)} %refs_0_.3) | copy-start | bytes 3145732
  2.8 11.6 %collective-permute-start.4 = (f32[256,16]{0,1:T(8,128)S(1)}, f32[256,16]{0,1:T(8,128)S(1)}, u32[]{:S(2)}, u32[]{:S(2)}) collective-permute-start(f32[256,16]{0,1:T(8,128)S(1)} %get-tuple-element.20), channel_id=1, source_target_pairs={{0,2},{1,3},{2,0},{3,1},{4,6},{5,7},{6,4},{7,5}} | collective-permute-start | bytes 49160 | tf_op jit(solution)/shard_map/ppermute | solution.py:20
  6.2 8.3 %collective-permute-start.3 = (f32[256,16]{0,1:T(8,128)S(1)}, f32[256,16]{0,1:T(8,128)S(1)}, u32[]{:S(2)}, u32[]{:S(2)}) collective-permute-start(f32[256,16]{0,1:T(8,128)S(1)} %get-tuple-element.20), channel_id=1, source_target_pairs={{0,1},{1,0},{2,3},{3,2},{4,5},{5,4},{6,7},{7,6}} | collective-permute-start | bytes 49160 | tf_op jit(solution)/shard_map/ppermute | solution.py:20
  12.1 36.6 %copy-start.4 = (bf16[256,2048]{1,0:T(8,128)(2,1)}, bf16[256,2048]{1,0:T(8,128)(2,1)S(1)}, u32[]{:S(2)}) copy-start(bf16[256,2048]{1,0:T(8,128)(2,1)S(1)} %fusion.2.refs_4_.refs_0_) | copy-start | bytes 3145732
  12.1 26.2 %collective-permute-start.7 = (bf16[256,2048]{1,0:T(8,128)(2,1)S(1)}, bf16[256,2048]{1,0:T(8,128)(2,1)}, u32[]{:S(2)}, u32[]{:S(2)}) collective-permute-start(bf16[256,2048]{1,0:T(8,128)(2,1)S(1)} %fusion.2.refs_4_.refs_0_), channel_id=1, source_target_pairs={{0,2},{1,3},{2,0},{3,1},{4,6},{5,7},{6,4},{7,5}} | collective-permute-start | bytes 3145736 | tf_op jit(solution)/shard_map/ppermute | solution.py:20
  12.3 48.7 %collective-permute-start.6 = (bf16[256,2048]{1,0:T(8,128)(2,1)S(1)}, bf16[256,2048]{1,0:T(8,128)(2,1)}, u32[]{:S(2)}, u32[]{:S(2)}) collective-permute-start(bf16[256,2048]{1,0:T(8,128)(2,1)S(1)} %fusion.2.refs_4_.refs_0_), channel_id=1, source_target_pairs={{0,1},{1,0},{2,3},{3,2},{4,5},{5,4},{6,7},{7,6}} | collective-permute-start | bytes 3145736 | tf_op jit(solution)/shard_map/ppermute | solution.py:20
  12.7 47.8 %collective-permute-start.1 = (bf16[256,2048]{1,0:T(8,128)(2,1)S(1)}, bf16[256,2048]{1,0:T(8,128)(2,1)S(1)}, u32[]{:S(2)}, u32[]{:S(2)}) collective-permute-start(bf16[256,2048]{1,0:T(8,128)(2,1)S(1)} %copy-done.2), channel_id=1, source_target_pairs={{0,2},{1,3},{2,0},{3,1},{4,6},{5,7},{6,4},{7,5}} | collective-permute-start | bytes 3145736 | tf_op jit(solution)/shard_map/ppermute | solution.py:20
  14.4 1.2 collective-permute-start.5
  14.5 79.7 %collective-permute-start = (bf16[256,2048]{1,0:T(8,128)(2,1)S(1)}, bf16[256,2048]{1,0:T(8,128)(2,1)}, u32[]{:S(2)}, u32[]{:S(2)}) collective-permute-start(bf16[256,2048]{1,0:T(8,128)(2,1)S(1)} %copy-done.2), channel_id=1, source_target_pairs={{0,1},{1,0},{2,3},{3,2},{4,5},{5,4},{6,7},{7,6}} | collective-permute-start | bytes 3145736 | tf_op jit(solution)/shard_map/ppermute | solution.py:20
  38.3 22.7 %collective-permute-start.8 = (bf16[256,2048]{1,0:T(8,128)(2,1)}, bf16[256,2048]{1,0:T(8,128)(2,1)}, u32[]{:S(2)}, u32[]{:S(2)}) collective-permute-start(bf16[256,2048]{1,0:T(8,128)(2,1)} %collective-permute-done.7.refs_6_.refs_2_), channel_id=1, source_target_pairs={{0,1},{1,0},{2,3},{3,2},{4,5},{5,4},{6,7},{7,6}} | collective-permute-start | bytes 3145736 | tf_op jit(solution)/shard_map/ppermute | solution.py:20
  39.1 0.6 copy-start.14
  55.7 3.6 copy-start.11
  55.7 3.6 copy-start.12
  55.7 3.7 copy-start.13
  60.5 33.7 %copy-start.6 = (bf16[256,2048]{1,0:T(8,128)(2,1)}, bf16[256,2048]{1,0:T(8,128)(2,1)S(1)}, u32[]{:S(2)}) copy-start(bf16[256,2048]{1,0:T(8,128)(2,1)S(1)} %collective-permute-done.1.refs_2_) | copy-start | bytes 3145732
  60.5 33.7 %collective-permute-start.2 = (bf16[256,2048]{1,0:T(8,128)(2,1)S(1)}, bf16[256,2048]{1,0:T(8,128)(2,1)}, u32[]{:S(2)}, u32[]{:S(2)}) collective-permute-start(bf16[256,2048]{1,0:T(8,128)(2,1)S(1)} %collective-permute-done.1.refs_2_), channel_id=1, source_target_pairs={{0,1},{1,0},{2,3},{3,2},{4,5},{5,4},{6,7},{7,6}} | collective-permute-start | bytes 3145736 | tf_op jit(solution)/shard_map/ppermute | solution.py:20
  196.5 3.4 copy-start.9
  199.9 92.8 %collective-permute-start.15 = (f32[2,256,1024]{2,1,0:T(8,128)}, f32[2,256,1024]{2,1,0:T(8,128)}, u32[]{:S(2)}, u32[]{:S(2)}) collective-permute-start(f32[2,256,1024]{2,1,0:T(8,128)} %slice.112), channel_id=1, source_target_pairs={{0,1},{1,0},{2,3},{3,2},{4,5},{5,4},{6,7},{7,6}} | collective-permute-start | bytes 6291464 | tf_op jit(solution)/shard_map/ppermute | solution.py:20
  201.3 93.4 %collective-permute-start.13 = (f32[2,256,1024]{2,1,0:T(8,128)}, f32[2,256,1024]{2,1,0:T(8,128)}, u32[]{:S(2)}, u32[]{:S(2)}) collective-permute-start(f32[2,256,1024]{2,1,0:T(8,128)} %slice.106), channel_id=1, source_target_pairs={{0,1},{1,0},{2,3},{3,2},{4,5},{5,4},{6,7},{7,6}} | collective-permute-start | bytes 6291464 | tf_op jit(solution)/shard_map/ppermute | solution.py:20
  263.2 35.3 %collective-permute-start.11 = (f32[2,256,1024]{2,1,0:T(8,128)S(1)}, f32[2,256,1024]{2,1,0:T(8,128)}, u32[]{:S(2)}, u32[]{:S(2)}) collective-permute-start(f32[2,256,1024]{2,1,0:T(8,128)S(1)} %slice.99), channel_id=1, source_target_pairs={{0,1},{1,0},{2,3},{3,2},{4,5},{5,4},{6,7},{7,6}} | collective-permute-start | bytes 6291464 | tf_op jit(solution)/shard_map/ppermute | solution.py:20
  290.2 2.8 copy-start.8
  292.1 6.4 %copy-start.7 = (f32[4,256,1024]{2,1,0:T(8,128)S(1)}, f32[4,256,1024]{2,1,0:T(8,128)}, u32[]{:S(2)}) copy-start(f32[4,256,1024]{2,1,0:T(8,128)} %shard_map.142) | copy-start | bytes 12582916
  292.1 7.9 %collective-permute-start.9 = (f32[2,256,1024]{2,1,0:T(8,128)S(1)}, f32[2,256,1024]{2,1,0:T(8,128)S(1)}, u32[]{:S(2)}, u32[]{:S(2)}) collective-permute-start(f32[2,256,1024]{2,1,0:T(8,128)S(1)} %slice.93), channel_id=1, source_target_pairs={{0,1},{1,0},{2,3},{3,2},{4,5},{5,4},{6,7},{7,6}} | collective-permute-start | bytes 6291464 | tf_op jit(solution)/shard_map/ppermute | solution.py:20
  294.7 5.4 %copy-start.10 = (f32[4,256,1024]{2,1,0:T(8,128)S(1)}, f32[4,256,1024]{2,1,0:T(8,128)}, u32[]{:S(2)}) copy-start(f32[4,256,1024]{2,1,0:T(8,128)} %shard_map.141) | copy-start | bytes 12582916
  294.7 26.2 %collective-permute-start.16 = (f32[256,1024]{1,0:T(8,128)S(1)}, f32[256,1024]{1,0:T(8,128)}, u32[]{:S(2)}, u32[]{:S(2)}) collective-permute-start(f32[256,1024]{1,0:T(8,128)S(1)} %fusion.3), channel_id=1, source_target_pairs={{0,2},{1,3},{2,0},{3,1},{4,6},{5,7},{6,4},{7,5}} | collective-permute-start | bytes 3145736 | tf_op jit(solution)/shard_map/ppermute | solution.py:20
  296.6 46.8 %collective-permute-start.14 = (f32[256,1024]{1,0:T(8,128)S(1)}, f32[256,1024]{1,0:T(8,128)}, u32[]{:S(2)}, u32[]{:S(2)}) collective-permute-start(f32[256,1024]{1,0:T(8,128)S(1)} %fusion.8), channel_id=1, source_target_pairs={{0,2},{1,3},{2,0},{3,1},{4,6},{5,7},{6,4},{7,5}} | collective-permute-start | bytes 3145736 | tf_op jit(solution)/shard_map/ppermute | solution.py:20
  299.9 66.0 %collective-permute-start.12 = (f32[256,1024]{1,0:T(8,128)S(1)}, f32[256,1024]{1,0:T(8,128)}, u32[]{:S(2)}, u32[]{:S(2)}) collective-permute-start(f32[256,1024]{1,0:T(8,128)S(1)} %fusion.13), channel_id=1, source_target_pairs={{0,2},{1,3},{2,0},{3,1},{4,6},{5,7},{6,4},{7,5}} | collective-permute-start | bytes 3145736 | tf_op jit(solution)/shard_map/ppermute | solution.py:20
  300.2 43.1 %copy-start.5 = (bf16[256,2048]{1,0:T(8,128)(2,1)S(1)}, bf16[256,2048]{1,0:T(8,128)(2,1)}, u32[]{:S(2)}) copy-start(bf16[256,2048]{1,0:T(8,128)(2,1)} %copy-done.4) | copy-start | bytes 3145732
  300.3 87.5 %collective-permute-start.10 = (f32[256,1024]{1,0:T(8,128)S(1)}, f32[256,1024]{1,0:T(8,128)}, u32[]{:S(2)}, u32[]{:S(2)}) collective-permute-start(f32[256,1024]{1,0:T(8,128)S(1)} %fusion.18), channel_id=1, source_target_pairs={{0,2},{1,3},{2,0},{3,1},{4,6},{5,7},{6,4},{7,5}} | collective-permute-start | bytes 3145736 | tf_op jit(solution)/shard_map/ppermute | solution.py:20
  315.1 72.6 %copy-start.3 = (bf16[256,2048]{1,0:T(8,128)(2,1)S(1)}, bf16[256,2048]{1,0:T(8,128)(2,1)}, u32[]{:S(2)}) copy-start(bf16[256,2048]{1,0:T(8,128)(2,1)} %refs_0_.3) | copy-start | bytes 3145732
  387.8 3.9 copy-start.1

commit v2 on v0

v2 whole, which is shorter than its diff:
```python
import functools

import jax
import jax.numpy as jnp
from jax import lax
from jax.experimental import pallas as pl
from jax.experimental.pallas import tpu as pltpu
from jax.sharding import PartitionSpec as P

F32 = jnp.float32
BF16 = jnp.bfloat16
CAP = 36
STRIDE = 32
WIN = 48
SLOTS = 144
CHUNK = 512
SET = 6
VMEM_LIMIT = 67043328


def dot(a, b):
    return jnp.dot(a, b, preferred_element_type=F32)


def layer_kernel(
    x_hbm, h_hbm, attn_hbm, meta_hbm, wqkv_hbm, wo_hbm, wg_hbm, wu_hbm, wd_hbm,
    mine_hbm, back_hbm, u_hbm, qkv_hbm,
    xv, xs, hh, ring, gm, mv, pt, zs, zr, xsend, mstage,
    ring_sem, tail_sem, load_sem, out_sem, meta_send, meta_recv, row_send, row_recv,
    zs_sem, zr_sem, xsend_sem, back_sem, mine_sem,
):
    tok, dim = x_hbm.shape
    local_n, ff, _ = wd_hbm.shape
    n_first = (local_n + 1) // 2
    n_both = local_n - n_first
    per = 5
    n_col = dim // CHUNK
    me = lax.axis_index('ep')
    sib = {'ep': me + 1 - 2 * lax.rem(me, 2)}
    peer = {'ep': lax.rem(me + 2, 4)}
    mesh_id = pl.DeviceIdType.MESH

    def remote(src, dst, send, recv, who):
        return pltpu.make_async_remote_copy(
            src_ref=src, dst_ref=dst, send_sem=send, recv_sem=recv, device_id=who, device_id_type=mesh_id)

    phases = {
        'o': 1, 'q': wqkv_hbm.shape[1] // (4 * CHUNK), 'ga': n_first, 'gab': n_both,
        'da': n_col * (local_n // per), 'gb': n_first, 'db': n_col * (local_n // per),
    }
    names = list(phases)
    base = {}
    total = 0
    for name in names:
        base[name] = total
        total += phases[name]

    def copies(name, i, half):
        s0 = half * SET
        out = []

        def add(src, slot, rows, lo, hi, sem):
            out.append(pltpu.make_async_copy(src, ring.at[s0 + slot, :rows, lo:hi], sem))

        if name in ('o', 'q'):
            for c in range(4):
                src = wo_hbm if name == 'o' else wqkv_hbm
                cols = pl.ds(pl.multiple_of((4 * i + c) * CHUNK, CHUNK), CHUNK)
                add(src.at[:, cols], c, dim, 0, CHUNK, ring_sem.at[half, c])
        elif name[0] == 'g':
            e = i + (n_first if name == 'gab' else 0)
            for p in range(2):
                cols = slice(p * CHUNK, (p + 1) * CHUNK)
                add(wg_hbm.at[e, :, cols], 2 * p, dim, 0, CHUNK, ring_sem.at[half, 2 * p])
                add(wu_hbm.at[e, :, cols], 2 * p + 1, dim, 0, CHUNK, ring_sem.at[half, 2 * p + 1])
            add(wg_hbm.at[e, :, 1024:1408], 4, dim, 0, 384, ring_sem.at[half, 4])
            add(wu_hbm.at[e, :, 1280:1408], 4, dim, 384, 512, tail_sem.at[half])
            add(wu_hbm.at[e, :, 1024:1280], 5, dim, 0, 256, ring_sem.at[half, 5])
        else:
            j, q = i // (local_n // per), lax.rem(i, local_n // per)
            cols = pl.ds(pl.multiple_of(j * CHUNK, CHUNK), CHUNK)
            for c in range(per):
                add(wd_hbm.at[q * per + c, :, cols], c, ff, 0, CHUNK, ring_sem.at[half, c])
        return out

    def start(name, i, half):
        for c in copies(name, i, half):
            c.start()

    def wait(name, i, half):
        for c in copies(name, i, half):
            c.wait()

    def half_of(name, i):
        return lax.rem(base[name] + i, 2)

    def prefetch(name, i):
        n = phases[name]
        half = half_of(name, i)
        at = names.index(name)

        def later(k):
            if at + 1 < len(names):
                start(names[at + 1], k, half)

        if isinstance(i, int):
            if i + 2 < n:
                start(name, i + 2, half)
            else:
                later(i + 2 - n)
        else:
            @pl.when(i + 2 < n)
            def _():
                start(name, i + 2, half)

            @pl.when(i + 2 >= n)
            def _():
                later(i + 2 - n)

    barrier = pltpu.get_barrier_semaphore()
    for who in (sib, peer):
        pl.semaphore_signal(barrier, inc=1, device_id=who, device_id_type=mesh_id)
    pl.semaphore_wait(barrier, 2)

    loads = [
        pltpu.make_async_copy(attn_hbm, xs.at[0:tok], load_sem.at[0]),
        pltpu.make_async_copy(h_hbm, xs.at[tok:2 * tok], load_sem.at[1]),
        pltpu.make_async_copy(x_hbm, xv.at[0, 0], load_sem.at[2]),
        pltpu.make_async_copy(meta_hbm, mv.at[0], load_sem.at[3]),
    ]
    for c in loads[:2]:
        c.start()
    start('o', 0, 0)
    meta_out = [remote(meta_hbm, mv.at[2], meta_send.at[0], meta_recv.at[0], peer),
                remote(meta_hbm, mv.at[1], meta_send.at[1], meta_recv.at[1], sib)]
    rows_out = [remote(x_hbm, xv.at[0, 2], row_send.at[0, 0], row_recv.at[0, 0], peer),
                remote(x_hbm, xv.at[0, 1], row_send.at[0, 1], row_recv.at[0, 1], sib)]
    for c in meta_out + rows_out:
        c.start()
    for c in loads[2:]:
        c.start()
    start('q', 0, 1)
    for c in loads[:2]:
        c.wait()

    wait('o', 0, 0)
    for c in range(4):
        cols = slice(c * CHUNK, (c + 1) * CHUNK)
        proj = dot(xs[0:tok, :], ring[c]).astype(BF16)
        xv[1, 0, :, cols] = (xs[tok:2 * tok, cols].astype(F32) + proj.astype(F32)).astype(BF16)
    prefetch('o', 0)

    n_q = phases['q']

    def qkv_out(i):
        rows = pl.ds(pl.multiple_of((2 + lax.rem(i, 2)) * tok, tok), tok)
        cols = pl.ds(pl.multiple_of(i * 4 * CHUNK, 4 * CHUNK), 4 * CHUNK)
        return pltpu.make_async_copy(xs.at[rows], qkv_hbm.at[:, cols], out_sem.at[lax.rem(i, 2)])

    def qkv_step(i, carry):
        half = half_of('q', i)
        wait('q', i, half)

        @pl.when(i >= 2)
        def _():
            qkv_out(i - 2).wait()

        rows = pl.ds(pl.multiple_of((2 + lax.rem(i, 2)) * tok, tok), tok)
        for c in range(4):
            out = dot(xs[tok:2 * tok, :], ring[half * SET + c])
            xs[rows, c * CHUNK:(c + 1) * CHUNK] = out.astype(BF16)
        prefetch('q', i)
        qkv_out(i).start()
        return carry

    lax.fori_loop(0, 1, qkv_step, 0)
    u_out = pltpu.make_async_copy(xv.at[1, 0], u_hbm, out_sem.at[2])
    u_out.start()
    rows_out += [remote(xv.at[1, 0], xv.at[1, 2], row_send.at[1, 0], row_recv.at[1, 0], peer),
                 remote(xv.at[1, 0], xv.at[1, 1], row_send.at[1, 1], row_recv.at[1, 1], sib)]
    for c in rows_out[2:]:
        c.start()
    lax.fori_loop(1, n_q, qkv_step, 0)

    meta_out[0].wait_recv()
    meta_out.append(remote(mv.at[2], mv.at[3], meta_send.at[2], meta_recv.at[2], sib))
    meta_out[2].start()
    loads[3].wait()
    meta_out[1].wait_recv()
    meta_out[2].wait_recv()
    for c in meta_out:
        c.wait_send()
    first_expert = (me * local_n).astype(F32)
    expert_rows = lax.broadcasted_iota(jnp.int32, (16, tok), 0).astype(F32)
    before = (lax.broadcasted_iota(jnp.int32, (tok, tok), 0)
              < lax.broadcasted_iota(jnp.int32, (tok, tok), 1)).astype(F32).astype(BF16)
    for k in range(4):
        turned = mv[k].T
        for m in range(2):
            hit = jnp.zeros((16, tok), F32)
            for c in range(4):
                local = turned[4 * m + c:4 * m + c + 1, :] - first_expert
                hit = jnp.where(jnp.broadcast_to(local, (16, tok)) == expert_rows, 1.0, hit)
            rank = dot(hit.astype(BF16), before)
            pt[m, k] = jnp.where(hit > 0.5, rank + 4.0 * k, -1.0)

    def mix_tables(m):
        lanes = gm.shape[3]
        col = lax.broadcasted_iota(jnp.int32, (16, lanes), 1)
        first = WIN * lax.broadcasted_iota(jnp.int32, (16, lanes), 0)
        inside = (col >= first) & (col < first + WIN)
        expand = jnp.where(inside, 1.0, 0.0).astype(BF16)
        offset = jnp.sum(jnp.where(inside, (col - first).astype(F32), 0.0), axis=0, keepdims=True)
        expert_lanes = lax.broadcasted_iota(jnp.int32, (tok, 16), 1).astype(F32)
        after = (lax.broadcasted_iota(jnp.int32, (tok, tok), 0)
                 > lax.broadcasted_iota(jnp.int32, (tok, tok), 1)).astype(F32).astype(BF16)
        for k in range(4):
            hit = jnp.zeros((tok, 16), F32)
            gate = jnp.zeros((tok, 16), F32)
            for c in range(4):
                local = mv[k, :, 4 * m + c:4 * m + c + 1] - first_expert
                same = jnp.broadcast_to(local, (tok, 16)) == expert_lanes
                hit = jnp.where(same, 1.0, hit)
                gate = jnp.where(same, jnp.broadcast_to(mv[k, :, 8 + 4 * m + c:9 + 4 * m + c], (tok, 16)), gate)
            place = jnp.where(hit > 0.5, dot(after, hit.astype(BF16)) + 4.0 * k, -1.0)
            here = dot(place.astype(BF16), expand) == offset
            for i in range(3):
                part = gate.astype(BF16)
                gate = gate - part.astype(F32)
                gm[k, i] = jnp.where(here, dot(part, expand), 0.0).astype(BF16)

    def dispatch(m, k, e0, ne, rows_per, shift):
        rows = lax.broadcasted_iota(jnp.int32, (WIN, tok), 0).astype(F32)
        pick = jnp.concatenate([
            jnp.where(jnp.broadcast_to(pt[m, k, e:e + 1, :], (WIN, tok)) == rows, 1.0, 0.0).astype(BF16)
            for e in range(e0, e0 + ne)], axis=0)
        for c in range(0, dim, CHUNK):
            got = dot(pick, xv[m, k, :, c:c + CHUNK]).astype(BF16)
            for e in range(ne):
                lo = e * rows_per + shift + STRIDE * k
                piece = got[e * WIN:(e + 1) * WIN]
                if k == 0:
                    xs[lo:lo + WIN, c:c + CHUNK] = piece
                else:
                    xs[lo:lo + 16, c:c + CHUNK] += piece[:16]
                    xs[lo + 16:lo + WIN, c:c + CHUNK] = piece[16:]

    def gate_up(name, rows_per, where):
        def step(i, carry):
            half = half_of(name, i)
            s0 = half * SET
            wait(name, i, half)
            rows = pl.ds(pl.multiple_of(i * rows_per, 16), rows_per)

            def put(lo, hi, g, u):
                h = (jax.nn.silu(g) * u).astype(BF16)
                for r, shift in enumerate(where):
                    hh[i + shift, :, lo:hi] = h[r * SLOTS:(r + 1) * SLOTS]

            for p in range(2):
                g = dot(xs[rows, :], ring[s0 + 2 * p])
                u = dot(xs[rows, :], ring[s0 + 2 * p + 1])
                put(p * CHUNK, (p + 1) * CHUNK, g, u)
            t = dot(xs[rows, :], ring[s0 + 4])
            u = dot(xs[rows, :], ring[s0 + 5, :, 0:256])
            put(1024, 1280, t[:, :256], u)
            put(1280, 1408, t[:, 256:384], t[:, 384:512])
            prefetch(name, i)
            return carry

        lax.fori_loop(0, phases[name], step, 0)

    def mine_out(m, j):
        slot = lax.rem(j, 2)
        cols = pl.ds(pl.multiple_of(j * CHUNK, CHUNK), CHUNK)
        return pltpu.make_async_copy(mstage.at[slot], mine_hbm.at[m, :, cols], mine_sem.at[slot])

    def back_out(m, j):
        slot = lax.rem(j, 2)
        cols = pl.ds(pl.multiple_of(j * CHUNK, CHUNK), CHUNK)
        return remote(xsend.at[slot], back_hbm.at[m, :, cols], xsend_sem.at[slot], back_sem.at[m, j], peer)

    def sib_out(j):
        slot = lax.rem(j, 2)
        return remote(zs, zr.at[slot], zs_sem, zr_sem.at[slot], sib)

    def down(name, m):
        groups = local_n // per

        def step(i, carry):
            half = half_of(name, i)
            s0 = half * SET
            j, q = i // groups, lax.rem(i, groups)
            wait(name, i, half)
            for c in range(per):
                e = q * per + c
                y = dot(hh[e + m * n_both], ring[s0 + c, :ff, :])
                xs[pl.ds(pl.multiple_of(e * SLOTS, 16), SLOTS), 0:CHUNK] = y.astype(BF16)
            prefetch(name, i)

            @pl.when(q == groups - 1)
            def _():
                slot = lax.rem(j, 2)

                def mix(k):
                    y = jnp.concatenate(
                        [xs[e * SLOTS + STRIDE * k:e * SLOTS + STRIDE * k + WIN, 0:CHUNK] for e in range(local_n)], axis=0)
                    return dot(gm[k, 0], y) + dot(gm[k, 1], y) + dot(gm[k, 2], y)

                if m == 0:
                    @pl.when(j >= 1)
                    def _():
                        sib_out(j - 1).wait_send()

                    @pl.when(j >= 2)
                    def _():
                        mine_out(0, j - 2).wait()
                        back_out(0, j - 2).wait_send()
                else:
                    sib_out(j + 1).wait_send()
                    mine_out(m, j).wait()
                    back_out(m, j).wait_send()
                zs[0] = mix(1)
                zs[1] = mix(3)
                sib_out(j).start()
                mstage[slot] = mix(0)
                xsend[slot] = mix(2)
                sib_out(j).wait_recv()
                mstage[slot] = mstage[slot] + zr[slot, 0]
                xsend[slot] = xsend[slot] + zr[slot, 1]
                back_out(m, j).start()
                mine_out(m, j).start()

            return carry

        lax.fori_loop(0, phases[name], step, 0)

    def forward(m):
        rows_out[2 * m].wait_recv()
        c = remote(xv.at[m, 2], xv.at[m, 3], row_send.at[m, 2], row_recv.at[m, 2], sib)
        c.start()
        return c

    for i in (n_q - 2, n_q - 1):
        qkv_out(i).wait()
    loads[2].wait()
    rows_out[1].wait_recv()
    dispatch(0, 0, 0, n_first, SLOTS, 0)
    dispatch(0, 1, 0, n_first, SLOTS, 0)
    forward_a = forward(0)
    dispatch(0, 2, 0, n_first, SLOTS, 0)
    forward_a.wait_recv()
    dispatch(0, 3, 0, n_first, SLOTS, 0)
    gate_up('ga', SLOTS, (0,))
    for k in range(4):
        dispatch(0, k, n_first, n_both, 2 * SLOTS, 0)
    rows_out[3].wait_recv()
    dispatch(1, 0, n_first, n_both, 2 * SLOTS, SLOTS)
    dispatch(1, 1, n_first, n_both, 2 * SLOTS, SLOTS)
    forward_b = forward(1)
    dispatch(1, 2, n_first, n_both, 2 * SLOTS, SLOTS)
    mix_tables(0)
    forward_b.wait_recv()
    dispatch(1, 3, n_first, n_both, 2 * SLOTS, SLOTS)
    gate_up('gab', 2 * SLOTS, (n_first, n_first + n_both))
    down('da', 0)
    for k in range(4):
        dispatch(1, k, 0, n_first, SLOTS, 0)
    gate_up('gb', SLOTS, (n_both,))
    mix_tables(1)
    down('db', 1)

    for c in rows_out + [forward_a, forward_b]:
        c.wait_send()
    u_out.wait()
    sib_out(n_col - 1).wait_send()
    for j in (n_col - 2, n_col - 1):
        mine_out(1, j).wait()
        back_out(1, j).wait_send()
    for m in range(2):
        for j in range(n_col):
            back_out(m, j).wait_recv()


def moe_layer(x_a, h_b, attn_b, meta, w_qkv, w_o, w_gate, w_up, w_down):
    tok, dim = x_a.shape
    local_n, ff, _ = w_down.shape
    n_both = local_n - (local_n + 1) // 2
    hbm = pl.BlockSpec(memory_space=pl.ANY)
    dma = pltpu.SemaphoreType.DMA
    flops = 2 * tok * dim * (dim + w_qkv.shape[1]) + local_n * 2 * SLOTS * 6 * dim * ff
    return pl.pallas_call(
        layer_kernel,
        in_specs=[hbm] * 9,
        out_specs=[hbm] * 4,
        out_shape=[
            jax.ShapeDtypeStruct((2, tok, dim), F32),
            jax.ShapeDtypeStruct((2, tok, dim), F32),
            jax.ShapeDtypeStruct((tok, dim), BF16),
            jax.ShapeDtypeStruct((tok, w_qkv.shape[1]), BF16),
        ],
        scratch_shapes=[
            pltpu.VMEM((2, 4, tok, dim), BF16),
            pltpu.VMEM((local_n * SLOTS, dim), BF16),
            pltpu.VMEM((local_n + n_both, SLOTS, ff), BF16),
            pltpu.VMEM((2 * SET, dim, CHUNK), BF16),
            pltpu.VMEM((4, 3, tok, local_n * WIN), BF16),
            pltpu.VMEM((4, tok, 128), F32),
            pltpu.VMEM((2, 4, 16, tok), F32),
            pltpu.VMEM((2, tok, CHUNK), F32),
            pltpu.VMEM((2, 2, tok, CHUNK), F32),
            pltpu.VMEM((2, tok, CHUNK), F32),
            pltpu.VMEM((2, tok, CHUNK), F32),
            dma((2, SET)), dma((2,)), dma((4,)), dma((3,)), dma((3,)), dma((3,)), dma((2, 3)), dma((2, 3)),
            dma(()), dma((2,)), dma((2,)), dma((2, dim // CHUNK)), dma((2,)),
        ],
        compiler_params=pltpu.CompilerParams(
            collective_id=0, has_side_effects=True, vmem_limit_bytes=VMEM_LIMIT),
        cost_estimate=pl.CostEstimate(flops=flops, bytes_accessed=local_n * 6 * dim * ff, transcendentals=0),
        name='moe_layer',
    )(x_a, h_b, attn_b, meta, w_qkv, w_o, w_gate, w_up, w_down)


def solution(mesh):
    def local_step(x_a, route_a, gate_a, h_b, attn_b, route_b, gate_b, w_qkv, w_o, w_gate, w_up, w_down):
        meta = jnp.concatenate([route_a.astype(F32), route_b.astype(F32), gate_a, gate_b], axis=1)
        meta = jnp.pad(meta, ((0, 0), (0, 128 - meta.shape[1])))
        mine, back, u_b, qkv_b = moe_layer(x_a, h_b, attn_b, meta, w_qkv, w_o, w_gate, w_up, w_down)
        out_a = (x_a.astype(F32) + (mine[0] + back[0])).astype(BF16)
        out_b = (u_b.astype(F32) + (mine[1] + back[1])).astype(BF16)
        return out_a, out_b, qkv_b

    row_spec = P(('dp', 'ep'), None)
    full_spec = P(None, None)
    expert_spec = P('ep', None, None)
    return jax.shard_map(
        local_step,
        mesh=mesh,
        in_specs=(row_spec, row_spec, row_spec, row_spec, row_spec, row_spec, row_spec, full_spec, full_spec, expert_spec, expert_spec, expert_spec),
        out_specs=(row_spec, row_spec, row_spec),
        check_vma=False,
    )
```

time: 656 us -> 230 us (0.35); the launches traced: 645 us -> 229 us
  matrix products: 341 us -> 0 us
  Pallas kernels: 0 us -> 217 us
  local copies, waits for them, and re-layouts: 130 us -> 2.44 us
  waiting for transfers between devices: 105 us -> 0 us
  other arithmetic: 43.1 us -> 8.76 us
  starting transfers between devices: 24.5 us -> 0 us
    dot_general x12 -> x0, matrix products: 341 us -> none  [the longest x2 109 us: expert_ffn(): jnp.einsum('erd,edf->erf', rows_in, w_gate, preferred_element_type=jnp.fl...]
    pallas_call x0 -> x1, Pallas kernels: none -> 217 us  [moe_layer(): pl.pallas_call(layer_kernel, in_specs=[hbm] * 9, out_specs=[hbm] * 4, out...]
    all_to_all x4 -> x0, waiting for transfers between devices: 105 us -> none  [the longest x2 53.9 us: moe_local(): recv_buf = lax.all_to_all(send_buf, 'ep', 1, 1, tiled=True)]
    reshape x6 -> x0, local copies, waits for them, and re-layouts: 75.1 us -> none  [the longest x4 50 us: moe_local(): send_buf = send_buf.reshape(local_n, n_devs, capacity, model_dim)]
    another operation x4 -> x0, other arithmetic: 33.8 us -> none
    all_to_all x2 -> x0, local copies, waits for them, and re-layouts: 25.6 us -> none  [moe_local(): lax.all_to_all(expert_out.reshape(local_n, n_devs, capacity, model_dim),...]
    all_to_all x4 -> x0, starting transfers between devices: 24.5 us -> none  [the longest x2 12.3 us: moe_local(): recv_buf = lax.all_to_all(send_buf, 'ep', 1, 1, tiled=True)]
    convert_element_type x2 -> x0, local copies, waits for them, and re-layouts: 24.2 us -> none  [expert_ffn(): jnp.einsum('erf,efd->erd', hidden, w_down, preferred_element_type=jnp.flo...]
  transfers between devices with their start and end apart: 4 -> 0, of which waited for: 2 -> 0; matrix products, arithmetic and copies ran while one was open for 64% -> 0% of each run, Pallas kernels for 0% -> 0%
where the time goes in v2:
time: 230 us; the launch traced here: 229 us
  Pallas kernels  217 us (94%)
  other arithmetic  8.76 us (4%)
  local copies, waits for them, and re-layouts  2.44 us (1%)
    pallas_call x1, Pallas kernels, moe_layer(): pl.pallas_call(layer_kernel, in_specs=[hbm] * 9, out_specs=[hbm] * 4, out...  217 us
    convert_element_type x1, other arithmetic, local_step(): out_b = (u_b.astype(F32) + (mine[1] + back[1])).astype(BF16)  6.67 us

profile of v2, /device:TPU:0, one launch (start us, length us, event | category | flops | bytes accessed | tf_op | source)
XLA Modules:
  0.0 229.3 jit_solution(3367109731899146340)
XLA Ops:
  0.6 0.7 convert_element_type.21
  1.3 0.7 convert_element_type.22
  2.0 0.7 pad_maximum_fusion
  2.7 0.1 copy.19
  2.8 0.7 pad.4.meta_hbm
  3.5 217.5 %moe_layer.1 = (f32[2,256,2048]{2,1,0:T(8,128)}, f32[2,256,2048]{2,1,0:T(8,128)}, bf16[256,2048]{1,0:T(8,128)(2,1)}, bf16[256,6144]{1,0:T(8,128)(2,1)}) custom-call(bf16[256,2048]{1,0:T(8,128)(2,1)} %x_hbm.1, bf16[256,2048]{1,0:T(8,128)(2,1)} %h_hbm.1, bf16[256,2048]{1,0:T(8,128)(2,1)} %attn_hbm.1, f32[256,128]{1,0:T(8,128)} %pad.4.meta_hbm, ...), custom_call_target="tpu_custom_call" | custom-call | flops 83332431872 | bytes 259522560 | tf_op jit(solution)/shard_map/moe_layer/pallas_call | solution.py:392
  221.0 0.0 copy-start
  221.0 6.7 %fusion = (bf16[256,2048]{1,0:T(8,128)(2,1)}, bf16[256,2048]{1,0:T(8,128)(2,1)}) fusion(f32[2,256,2048]{2,1,0:T(8,128)} %get-tuple-element.8, f32[2,256,2048]{2,1,0:T(8,128)} %get-tuple-element.7, bf16[256,2048]{1,0:T(8,128)(2,1)} %get-tuple-element.9, bf16[256,2048]{1,0:T(8,128)(2,1)} %x_hbm.1), kind=kLoop, calls=%fused_computation.1 | loop fusion | flops 4194304 | bytes 12582912 | tf_op jit(solution)/shard_map/convert_element_type | solution.py:430
  227.7 0.0 copy-done
  227.7 1.7 copy.21
Async XLA Ops:
  221.0 6.7 %copy-start = (bf16[256,6144]{1,0:T(8,128)(2,1)S(1)}, bf16[256,6144]{1,0:T(8,128)(2,1)}, u32[]{:S(2)}) copy-start(bf16[256,6144]{1,0:T(8,128)(2,1)} %get-tuple-element.18) | copy-start | bytes 9437188

commit v3 on v2

--- a/solution.py
+++ b/solution.py
@@ -24,10 +24,10 @@
 
 def layer_kernel(
     x_hbm, h_hbm, attn_hbm, meta_hbm, wqkv_hbm, wo_hbm, wg_hbm, wu_hbm, wd_hbm,
-    mine_hbm, back_hbm, u_hbm, qkv_hbm,
+    mine_hbm, back_hbm, outa_hbm, outb_hbm, qkv_hbm,
     xv, xs, hh, ring, gm, mv, pt, zs, zr, xsend, mstage,
     ring_sem, tail_sem, load_sem, out_sem, meta_send, meta_recv, row_send, row_recv,
-    zs_sem, zr_sem, xsend_sem, back_sem, mine_sem,
+    zs_sem, zr_sem, xsend_sem, back_sem, mine_sem, last_sem, final_sem,
 ):
     tok, dim = x_hbm.shape
     local_n, ff, _ = wd_hbm.shape
@@ -46,8 +46,10 @@
 
     phases = {
         'o': 1, 'q': wqkv_hbm.shape[1] // (4 * CHUNK), 'ga': n_first, 'gab': n_both,
-        'da': n_col * (local_n // per), 'gb': n_first, 'db': n_col * (local_n // per),
+        'mix': n_col * (local_n // per) + n_first, 'db': n_col * (local_n // per),
     }
+    groups = local_n // per
+    each = n_first // n_col
     names = list(phases)
     base = {}
     total = 0
@@ -77,7 +79,7 @@
             add(wu_hbm.at[e, :, 1280:1408], 4, dim, 384, 512, tail_sem.at[half])
             add(wu_hbm.at[e, :, 1024:1280], 5, dim, 0, 256, ring_sem.at[half, 5])
         else:
-            j, q = i // (local_n // per), lax.rem(i, local_n // per)
+            j, q = i // groups, lax.rem(i, groups)
             cols = pl.ds(pl.multiple_of(j * CHUNK, CHUNK), CHUNK)
             for c in range(per):
                 add(wd_hbm.at[q * per + c, :, cols], c, ff, 0, CHUNK, ring_sem.at[half, c])
@@ -101,7 +103,7 @@
 
         def later(k):
             if at + 1 < len(names):
-                start(names[at + 1], k, half)
+                start({'mix': 'da'}.get(names[at + 1], names[at + 1]), k, half)
 
         if isinstance(i, int):
             if i + 2 < n:
@@ -121,6 +123,8 @@
     for who in (sib, peer):
         pl.semaphore_signal(barrier, inc=1, device_id=who, device_id_type=mesh_id)
     pl.semaphore_wait(barrier, 2)
+
+    base['da'] = base['mix']
 
     loads = [
         pltpu.make_async_copy(attn_hbm, xs.at[0:tok], load_sem.at[0]),
@@ -174,8 +178,6 @@
         return carry
 
     lax.fori_loop(0, 1, qkv_step, 0)
-    u_out = pltpu.make_async_copy(xv.at[1, 0], u_hbm, out_sem.at[2])
-    u_out.start()
     rows_out += [remote(xv.at[1, 0], xv.at[1, 2], row_send.at[1, 0], row_recv.at[1, 0], peer),
                  remote(xv.at[1, 0], xv.at[1, 1], row_send.at[1, 1], row_recv.at[1, 1], sib)]
     for c in rows_out[2:]:
@@ -195,14 +197,17 @@
     before = (lax.broadcasted_iota(jnp.int32, (tok, tok), 0)
               < lax.broadcasted_iota(jnp.int32, (tok, tok), 1)).astype(F32).astype(BF16)
     for k in range(4):
-        turned = mv[k].T
         for m in range(2):
             hit = jnp.zeros((16, tok), F32)
-            for c in range(4):
-                local = turned[4 * m + c:4 * m + c + 1, :] - first_expert
-                hit = jnp.where(jnp.broadcast_to(local, (16, tok)) == expert_rows, 1.0, hit)
+            gate = jnp.zeros((16, tok), F32)
+            for c in range(4 * m, 4 * m + 4):
+                local = mv[k, c:c + 1, :] - first_expert
+                same = jnp.broadcast_to(local, (16, tok)) == expert_rows
+                hit = jnp.where(same, 1.0, hit)
+                gate = jnp.where(same, jnp.broadcast_to(mv[k, 8 + c:9 + c, :], (16, tok)), gate)
             rank = dot(hit.astype(BF16), before)
-            pt[m, k] = jnp.where(hit > 0.5, rank + 4.0 * k, -1.0)
+            pt[0, m, k] = jnp.where(hit > 0.5, rank + 4.0 * k, -1.0)
+            pt[1, m, k] = gate
 
     def mix_tables(m):
         lanes = gm.shape[3]
@@ -211,19 +216,9 @@
         inside = (col >= first) & (col < first + WIN)
         expand = jnp.where(inside, 1.0, 0.0).astype(BF16)
         offset = jnp.sum(jnp.where(inside, (col - first).astype(F32), 0.0), axis=0, keepdims=True)
-        expert_lanes = lax.broadcasted_iota(jnp.int32, (tok, 16), 1).astype(F32)
-        after = (lax.broadcasted_iota(jnp.int32, (tok, tok), 0)
-                 > lax.broadcasted_iota(jnp.int32, (tok, tok), 1)).astype(F32).astype(BF16)
         for k in range(4):
-            hit = jnp.zeros((tok, 16), F32)
-            gate = jnp.zeros((tok, 16), F32)
-            for c in range(4):
-                local = mv[k, :, 4 * m + c:4 * m + c + 1] - first_expert
-                same = jnp.broadcast_to(local, (tok, 16)) == expert_lanes
-                hit = jnp.where(same, 1.0, hit)
-                gate = jnp.where(same, jnp.broadcast_to(mv[k, :, 8 + 4 * m + c:9 + 4 * m + c], (tok, 16)), gate)
-            place = jnp.where(hit > 0.5, dot(after, hit.astype(BF16)) + 4.0 * k, -1.0)
-            here = dot(place.astype(BF16), expand) == offset
+            here = dot(pt[0, m, k].T.astype(BF16), expand) == offset
+            gate = pt[1, m, k].T
             for i in range(3):
                 part = gate.astype(BF16)
                 gate = gate - part.astype(F32)
@@ -232,7 +227,7 @@
     def dispatch(m, k, e0, ne, rows_per, shift):
         rows = lax.broadcasted_iota(jnp.int32, (WIN, tok), 0).astype(F32)
         pick = jnp.concatenate([
-            jnp.where(jnp.broadcast_to(pt[m, k, e:e + 1, :], (WIN, tok)) == rows, 1.0, 0.0).astype(BF16)
+            jnp.where(jnp.broadcast_to(pt[0, m, k, e:e + 1, :], (WIN, tok)) == rows, 1.0, 0.0).astype(BF16)
             for e in range(e0, e0 + ne)], axis=0)
         for c in range(0, dim, CHUNK):
             got = dot(pick, xv[m, k, :, c:c + CHUNK]).astype(BF16)
@@ -245,35 +240,37 @@
                     xs[lo:lo + 16, c:c + CHUNK] += piece[:16]
                     xs[lo + 16:lo + WIN, c:c + CHUNK] = piece[16:]
 
+    def expert_hidden(i, half, rows_per, where):
+        s0 = half * SET
+        rows = pl.ds(pl.multiple_of(i * rows_per, 16), rows_per)
+
+        def put(lo, hi, g, u):
+            h = (jax.nn.silu(g) * u).astype(BF16)
+            for r, shift in enumerate(where):
+                hh[i + shift, :, lo:hi] = h[r * SLOTS:(r + 1) * SLOTS]
+
+        for p in range(2):
+            g = dot(xs[rows, :], ring[s0 + 2 * p])
+            u = dot(xs[rows, :], ring[s0 + 2 * p + 1])
+            put(p * CHUNK, (p + 1) * CHUNK, g, u)
+        t = dot(xs[rows, :], ring[s0 + 4])
+        u = dot(xs[rows, :], ring[s0 + 5, :, 0:256])
+        put(1024, 1280, t[:, :256], u)
+        put(1280, 1408, t[:, 256:384], t[:, 384:512])
+
     def gate_up(name, rows_per, where):
         def step(i, carry):
             half = half_of(name, i)
-            s0 = half * SET
             wait(name, i, half)
-            rows = pl.ds(pl.multiple_of(i * rows_per, 16), rows_per)
-
-            def put(lo, hi, g, u):
-                h = (jax.nn.silu(g) * u).astype(BF16)
-                for r, shift in enumerate(where):
-                    hh[i + shift, :, lo:hi] = h[r * SLOTS:(r + 1) * SLOTS]
-
-            for p in range(2):
-                g = dot(xs[rows, :], ring[s0 + 2 * p])
-                u = dot(xs[rows, :], ring[s0 + 2 * p + 1])
-                put(p * CHUNK, (p + 1) * CHUNK, g, u)
-            t = dot(xs[rows, :], ring[s0 + 4])
-            u = dot(xs[rows, :], ring[s0 + 5, :, 0:256])
-            put(1024, 1280, t[:, :256], u)
-            put(1280, 1408, t[:, 256:384], t[:, 384:512])
+            expert_hidden(i, half, rows_per, where)
             prefetch(name, i)
             return carry
 
         lax.fori_loop(0, phases[name], step, 0)
 
     def mine_out(m, j):
-        slot = lax.rem(j, 2)
         cols = pl.ds(pl.multiple_of(j * CHUNK, CHUNK), CHUNK)
-        return pltpu.make_async_copy(mstage.at[slot], mine_hbm.at[m, :, cols], mine_sem.at[slot])
+        return pltpu.make_async_copy(mstage, mine_hbm.at[m, :, cols], mine_sem)
 
     def back_out(m, j):
         slot = lax.rem(j, 2)
@@ -284,56 +281,109 @@
         slot = lax.rem(j, 2)
         return remote(zs, zr.at[slot], zs_sem, zr_sem.at[slot], sib)
 
-    def down(name, m):
-        groups = local_n // per
-
-        def step(i, carry):
-            half = half_of(name, i)
-            s0 = half * SET
-            j, q = i // groups, lax.rem(i, groups)
-            wait(name, i, half)
-            for c in range(per):
-                e = q * per + c
-                y = dot(hh[e + m * n_both], ring[s0 + c, :ff, :])
-                xs[pl.ds(pl.multiple_of(e * SLOTS, 16), SLOTS), 0:CHUNK] = y.astype(BF16)
-            prefetch(name, i)
-
-            @pl.when(q == groups - 1)
-            def _():
-                slot = lax.rem(j, 2)
-
-                def mix(k):
-                    y = jnp.concatenate(
-                        [xs[e * SLOTS + STRIDE * k:e * SLOTS + STRIDE * k + WIN, 0:CHUNK] for e in range(local_n)], axis=0)
-                    return dot(gm[k, 0], y) + dot(gm[k, 1], y) + dot(gm[k, 2], y)
-
-                if m == 0:
-                    @pl.when(j >= 1)
-                    def _():
-                        sib_out(j - 1).wait_send()
-
-                    @pl.when(j >= 2)
-                    def _():
-                        mine_out(0, j - 2).wait()
-                        back_out(0, j - 2).wait_send()
-                else:
-                    sib_out(j + 1).wait_send()
-                    mine_out(m, j).wait()
-                    back_out(m, j).wait_send()
-                zs[0] = mix(1)
-                zs[1] = mix(3)
-                sib_out(j).start()
-                mstage[slot] = mix(0)
-                xsend[slot] = mix(2)
-                sib_out(j).wait_recv()
-                mstage[slot] = mstage[slot] + zr[slot, 0]
-                xsend[slot] = xsend[slot] + zr[slot, 1]
-                back_out(m, j).start()
-                mine_out(m, j).start()
-
-            return carry
-
-        lax.fori_loop(0, phases[name], step, 0)
+    y_row = n_first * SLOTS
+    y_per = local_n - n_first
+
+    def expert_out(m, q, half):
+        for c in range(per):
+            e = q * per + c
+            y = dot(hh[e + m * local_n], ring[half * SET + c, :ff, :])
+            rows = pl.ds(pl.multiple_of(y_row + lax.rem(e, y_per) * SLOTS, 16), SLOTS)
+            cols = pl.ds(pl.multiple_of((e // y_per) * CHUNK, CHUNK), CHUNK)
+            xs[rows, cols] = y.astype(BF16)
+
+    def combine(m, j):
+        slot = lax.rem(j, 2)
+
+        def mix(k):
+            pieces = []
+            for e in range(local_n):
+                lo = y_row + (e % y_per) * SLOTS + STRIDE * k
+                c = (e // y_per) * CHUNK
+                pieces.append(xs[lo:lo + WIN, c:c + CHUNK])
+            y = jnp.concatenate(pieces, axis=0)
+            return dot(gm[k, 0], y) + dot(gm[k, 1], y) + dot(gm[k, 2], y)
+
+        if m == 0:
+            @pl.when(j >= 1)
+            def _():
+                sib_out(j - 1).wait_send()
+                mine_out(0, j - 1).wait()
+
+            @pl.when(j >= 2)
+            def _():
+                back_out(0, j - 2).wait_send()
+        else:
+            sib_out(j + 1).wait_send()
+            mine_out(m, j).wait()
+            back_out(m, j).wait_send()
+        zs[0] = mix(1)
+        zs[1] = mix(3)
+        sib_out(j).start()
+        mstage[...] = mix(0)
+        xsend[slot] = mix(2)
+        sib_out(j).wait_recv()
+        mstage[...] = mstage[...] + zr[slot, 0]
+        xsend[slot] = xsend[slot] + zr[slot, 1]
+        back_out(m, j).start()
+        mine_out(m, j).start()
+
+    def down_b(i, carry):
+        half = half_of('db', i)
+        wait('db', i, half)
+        expert_out(1, lax.rem(i, groups), half)
+        prefetch('db', i)
+
+        @pl.when(lax.rem(i, groups) == groups - 1)
+        def _():
+            combine(1, i // groups)
+
+        return carry
+
+    def down_a_gate_b(t, carry):
+        first = base['mix'] + t * (groups + each)
+
+        def outputs(q, c2):
+            half = lax.rem(first + q, 2)
+            wait('da', t * groups + q, half)
+            expert_out(0, q, half)
+
+            @pl.when(q + 2 < groups)
+            def _():
+                start('da', t * groups + q + 2, half)
+
+            @pl.when(q + 2 >= groups)
+            def _():
+                start('gb', t * each + q + 2 - groups, half)
+
+            return c2
+
+        lax.fori_loop(0, groups, outputs, 0)
+        combine(0, t)
+
+        @pl.when(t == 0)
+        def _():
+            for k in range(4):
+                dispatch(1, k, 0, n_first, SLOTS, 0)
+
+        def hidden(r, c2):
+            half = lax.rem(first + groups + r, 2)
+            e = t * each + r
+            wait('gb', e, half)
+            expert_hidden(e, half, SLOTS, (local_n,))
+
+            @pl.when(t + 1 < n_col)
+            def _():
+                start('da', (t + 1) * groups + r, half)
+
+            @pl.when(t + 1 >= n_col)
+            def _():
+                start('db', r, half)
+
+            return c2
+
+        lax.fori_loop(0, each, hidden, 0)
+        return carry
 
     def forward(m):
         rows_out[2 * m].wait_recv()
@@ -362,57 +412,72 @@
     mix_tables(0)
     forward_b.wait_recv()
     dispatch(1, 3, n_first, n_both, 2 * SLOTS, SLOTS)
-    gate_up('gab', 2 * SLOTS, (n_first, n_first + n_both))
-    down('da', 0)
-    for k in range(4):
-        dispatch(1, k, 0, n_first, SLOTS, 0)
-    gate_up('gb', SLOTS, (n_both,))
+    gate_up('gab', 2 * SLOTS, (n_first, local_n + n_first))
+    lax.fori_loop(0, n_col, down_a_gate_b, 0)
     mix_tables(1)
-    down('db', 1)
-
+    lax.fori_loop(0, phases['db'], down_b, 0)
+
+    sib_out(n_col - 1).wait_send()
+    mine_out(1, n_col - 1).wait()
+    for j in (n_col - 2, n_col - 1):
+        back_out(1, j).wait_send()
+    outs = []
+    for m in range(2):
+        for j in range(n_col):
+            slot = j % 2
+            cols = slice(j * CHUNK, (j + 1) * CHUNK)
+            back_out(m, j).wait_recv()
+            parts = [
+                pltpu.make_async_copy(mine_hbm.at[m, :, cols], zr.at[slot, 0], final_sem.at[0]),
+                pltpu.make_async_copy(back_hbm.at[m, :, cols], zr.at[slot, 1], final_sem.at[1]),
+            ]
+            for c in parts:
+                c.start()
+            for c in parts:
+                c.wait()
+            total_row = xv[m, 0, :, cols].astype(F32) + (zr[slot, 0] + zr[slot, 1])
+            xs[m * tok:(m + 1) * tok, cols] = total_row.astype(BF16)
+            out = pltpu.make_async_copy(
+                xs.at[m * tok:(m + 1) * tok, cols], (outa_hbm, outb_hbm)[m].at[:, cols], last_sem.at[m, j])
+            out.start()
+            outs.append(out)
     for c in rows_out + [forward_a, forward_b]:
         c.wait_send()
-    u_out.wait()
-    sib_out(n_col - 1).wait_send()
-    for j in (n_col - 2, n_col - 1):
-        mine_out(1, j).wait()
-        back_out(1, j).wait_send()
-    for m in range(2):
-        for j in range(n_col):
-            back_out(m, j).wait_recv()
+    for c in outs:
+        c.wait()
 
 
 def moe_layer(x_a, h_b, attn_b, meta, w_qkv, w_o, w_gate, w_up, w_down):
     tok, dim = x_a.shape
     local_n, ff, _ = w_down.shape
-    n_both = local_n - (local_n + 1) // 2
     hbm = pl.BlockSpec(memory_space=pl.ANY)
     dma = pltpu.SemaphoreType.DMA
     flops = 2 * tok * dim * (dim + w_qkv.shape[1]) + local_n * 2 * SLOTS * 6 * dim * ff
     return pl.pallas_call(
         layer_kernel,
         in_specs=[hbm] * 9,
-        out_specs=[hbm] * 4,
+        out_specs=[hbm] * 5,
         out_shape=[
             jax.ShapeDtypeStruct((2, tok, dim), F32),
             jax.ShapeDtypeStruct((2, tok, dim), F32),
+            jax.ShapeDtypeStruct((tok, dim), BF16),
             jax.ShapeDtypeStruct((tok, dim), BF16),
             jax.ShapeDtypeStruct((tok, w_qkv.shape[1]), BF16),
         ],
         scratch_shapes=[
             pltpu.VMEM((2, 4, tok, dim), BF16),
             pltpu.VMEM((local_n * SLOTS, dim), BF16),
-            pltpu.VMEM((local_n + n_both, SLOTS, ff), BF16),
+            pltpu.VMEM((2 * local_n, SLOTS, ff), BF16),
             pltpu.VMEM((2 * SET, dim, CHUNK), BF16),
             pltpu.VMEM((4, 3, tok, local_n * WIN), BF16),
-            pltpu.VMEM((4, tok, 128), F32),
-            pltpu.VMEM((2, 4, 16, tok), F32),
+            pltpu.VMEM((4, 16, tok), F32),
+            pltpu.VMEM((2, 2, 4, 16, tok), F32),
             pltpu.VMEM((2, tok, CHUNK), F32),
             pltpu.VMEM((2, 2, tok, CHUNK), F32),
             pltpu.VMEM((2, tok, CHUNK), F32),
-            pltpu.VMEM((2, tok, CHUNK), F32),
-            dma((2, SET)), dma((2,)), dma((4,)), dma((3,)), dma((3,)), dma((3,)), dma((2, 3)), dma((2, 3)),
-            dma(()), dma((2,)), dma((2,)), dma((2, dim // CHUNK)), dma((2,)),
+            pltpu.VMEM((tok, CHUNK), F32),
+            dma((2, SET)), dma((2,)), dma((4,)), dma((2,)), dma((3,)), dma((3,)), dma((2, 3)), dma((2, 3)),
+            dma(()), dma((2,)), dma((2,)), dma((2, dim // CHUNK)), dma(()), dma((2, dim // CHUNK)), dma((2,)),
         ],
         compiler_params=pltpu.CompilerParams(
             collective_id=0, has_side_effects=True, vmem_limit_bytes=VMEM_LIMIT),
@@ -423,11 +488,8 @@
 
 def solution(mesh):
     def local_step(x_a, route_a, gate_a, h_b, attn_b, route_b, gate_b, w_qkv, w_o, w_gate, w_up, w_down):
-        meta = jnp.concatenate([route_a.astype(F32), route_b.astype(F32), gate_a, gate_b], axis=1)
-        meta = jnp.pad(meta, ((0, 0), (0, 128 - meta.shape[1])))
-        mine, back, u_b, qkv_b = moe_layer(x_a, h_b, attn_b, meta, w_qkv, w_o, w_gate, w_up, w_down)
-        out_a = (x_a.astype(F32) + (mine[0] + back[0])).astype(BF16)
-        out_b = (u_b.astype(F32) + (mine[1] + back[1])).astype(BF16)
+        meta = jnp.concatenate([route_a.T.astype(F32), route_b.T.astype(F32), gate_a.T, gate_b.T], axis=0)
+        _, _, out_a, out_b, qkv_b = moe_layer(x_a, h_b, attn_b, meta, w_qkv, w_o, w_gate, w_up, w_down)
         return out_a, out_b, qkv_b
 
     row_spec = P(('dp', 'ep'), None)

time: 230 us -> 229 us (level)
  other arithmetic: 8.76 us -> 2.04 us
  local copies, waits for them, and re-layouts: 2.44 us -> 8.49 us
    convert_element_type x3 -> x1, other arithmetic: 8.05 us -> 0.72 us  [local_step(): route_b.T.astype(F32)]
    unnamed x3, local copies, waits for them, and re-layouts: 1.67 us -> 8.49 us
where the time goes in v3:
time: 229 us; the launch traced here: 228 us
  Pallas kernels  217 us (95%)
  local copies, waits for them, and re-layouts  8.49 us (4%)
    pallas_call x1, Pallas kernels, moe_layer(): pl.pallas_call(layer_kernel, in_specs=[hbm] * 9, out_specs=[hbm] * 5, out...  217 us
    unnamed x3, local copies, waits for them, and re-layouts  8.49 us

profile of v3, /device:TPU:0, one launch (start us, length us, event | category | flops | bytes accessed | tf_op | source)
XLA Modules:
  0.0 228.4 jit_solution(3505361103209807535)
XLA Ops:
  0.6 0.7 convert_bitcast_fusion
  1.4 1.3 pad_maximum_fusion.meta_hbm
  2.7 217.2 %moe_layer.1 = (f32[2,256,2048]{2,1,0:T(8,128)}, f32[2,256,2048]{2,1,0:T(8,128)}, bf16[256,2048]{1,0:T(8,128)(2,1)}, bf16[256,2048]{1,0:T(8,128)(2,1)}, bf16[256,6144]{1,0:T(8,128)(2,1)}) custom-call(bf16[256,2048]{1,0:T(8,128)(2,1)} %x_hbm.1, bf16[256,2048]{1,0:T(8,128)(2,1)} %h_hbm.1, bf16[256,2048]{1,0:T(8,128)(2,1)} %attn_hbm.1, ...), custom_call_target="tpu_custom_call" | custom-call | flops 83332431872 | bytes 259522560 | tf_op jit(solution)/shard_map/moe_layer/pallas_call | solution.py:456
  219.9 2.3 %copy.18 = bf16[256,2048]{1,0:T(8,128)(2,1)} copy(bf16[256,2048]{1,0:T(8,128)(2,1)} %get-tuple-element.14) | data formatting | bytes 2097152
  222.2 2.3 %copy.19 = bf16[256,2048]{1,0:T(8,128)(2,1)} copy(bf16[256,2048]{1,0:T(8,128)(2,1)} %get-tuple-element.15) | data formatting | bytes 2097152
  224.5 3.9 %copy.20 = bf16[256,6144]{1,0:T(8,128)(2,1)} copy(bf16[256,6144]{1,0:T(8,128)(2,1)} %get-tuple-element.16) | data formatting | bytes 6291456

commit v4 on v3

v4 whole, which is shorter than its diff:
```python
import functools

import jax
import jax.numpy as jnp
from jax import lax
from jax.experimental import pallas as pl
from jax.experimental.pallas import tpu as pltpu
from jax.sharding import PartitionSpec as P

F32 = jnp.float32
BF16 = jnp.bfloat16
CAP = 36
STRIDE = 32
WIN = 48
SLOTS = 144
CHUNK = 512
SET = 6
VMEM_LIMIT = 67043328


def dot(a, b):
    return jnp.dot(a, b, preferred_element_type=F32)


def layer_kernel(
    x_hbm, h_hbm, attn_hbm, ra_hbm, rb_hbm, ga_hbm, gb_hbm, wqkv_hbm, wo_hbm, wg_hbm, wu_hbm, wd_hbm,
    mine_hbm, back_hbm, outa_hbm, outb_hbm, qkv_hbm,
    xv, xs, hh, ring, gm, rv, gv, pt, zs, zr, xsend, mstage,
    ring_sem, tail_sem, load_sem, out_sem, meta_send, meta_recv, row_send, row_recv,
    zs_sem, zr_sem, xsend_sem, back_sem, mine_sem, last_sem, final_sem,
):
    tok, dim = x_hbm.shape
    local_n, ff, _ = wd_hbm.shape
    n_first = (local_n + 1) // 2
    n_both = local_n - n_first
    per = 5
    n_col = dim // CHUNK
    me = lax.axis_index('ep')
    sib = {'ep': me + 1 - 2 * lax.rem(me, 2)}
    peer = {'ep': lax.rem(me + 2, 4)}
    mesh_id = pl.DeviceIdType.MESH

    def remote(src, dst, send, recv, who):
        return pltpu.make_async_remote_copy(
            src_ref=src, dst_ref=dst, send_sem=send, recv_sem=recv, device_id=who, device_id_type=mesh_id)

    groups = local_n // per
    each = n_first // n_col
    n_q = wqkv_hbm.shape[1] // (4 * CHUNK)
    base_g = 1 + n_q
    base_mix = base_g + local_n
    base_db = base_mix + n_col * groups + n_first

    def half_at(it):
        return it % 2 if isinstance(it, int) else lax.rem(it, 2)

    def copies(kind, i, half, slots=range(SET)):
        out = []

        def add(src, slot, rows, lo, hi, sem):
            if slot in slots:
                out.append(pltpu.make_async_copy(src, ring.at[half, :rows, slot * CHUNK + lo:slot * CHUNK + hi], sem))

        if kind in ('o', 'q'):
            for c in range(4):
                src = wo_hbm if kind == 'o' else wqkv_hbm
                cols = pl.ds(pl.multiple_of((4 * i + c) * CHUNK, CHUNK), CHUNK)
                add(src.at[:, cols], c, dim, 0, CHUNK, ring_sem.at[half, c])
        elif kind == 'g':
            for p in range(2):
                cols = slice(p * CHUNK, (p + 1) * CHUNK)
                add(wg_hbm.at[i, :, cols], 2 * p, dim, 0, CHUNK, ring_sem.at[half, 2 * p])
                add(wu_hbm.at[i, :, cols], 2 * p + 1, dim, 0, CHUNK, ring_sem.at[half, 2 * p + 1])
            add(wg_hbm.at[i, :, 1024:1408], 4, dim, 0, 384, ring_sem.at[half, 4])
            add(wu_hbm.at[i, :, 1280:1408], 4, dim, 384, 512, tail_sem.at[half])
            add(wu_hbm.at[i, :, 1024:1280], 5, dim, 0, 256, ring_sem.at[half, 5])
        else:
            j, q = i
            cols = pl.ds(pl.multiple_of(j * CHUNK, CHUNK), CHUNK)
            for c in range(per):
                add(wd_hbm.at[q * per + c, :, cols], c, ff, 0, CHUNK, ring_sem.at[half, c])
        return out

    def start(*args):
        for c in copies(*args):
            c.start()

    def wait(*args):
        for c in copies(*args):
            c.wait()

    barrier = pltpu.get_barrier_semaphore()
    for who in (sib, peer):
        pl.semaphore_signal(barrier, inc=1, device_id=who, device_id_type=mesh_id)
    pl.semaphore_wait(barrier, 2)

    loads = [
        pltpu.make_async_copy(attn_hbm, xs.at[0:tok], load_sem.at[0]),
        pltpu.make_async_copy(h_hbm, xs.at[tok:2 * tok], load_sem.at[1]),
        pltpu.make_async_copy(x_hbm, xv.at[0, 0], load_sem.at[2]),
    ]
    meta = [(ra_hbm, rv, 0), (rb_hbm, rv, 1), (ga_hbm, gv, 0), (gb_hbm, gv, 1)]
    for i, (src, dst, m) in enumerate(meta):
        loads.append(pltpu.make_async_copy(src, dst.at[0, m], load_sem.at[3 + i]))
    for c in loads[:2]:
        c.start()
    start('o', 0, 0)
    meta_out = []
    for way, who, place in ((0, peer, 2), (1, sib, 1)):
        for i, (src, dst, m) in enumerate(meta):
            meta_out.append(remote(src, dst.at[place, m], meta_send.at[way, i], meta_recv.at[way, i], who))
    rows_out = [remote(x_hbm, xv.at[0, 2], row_send.at[0, 0], row_recv.at[0, 0], peer),
                remote(x_hbm, xv.at[0, 1], row_send.at[0, 1], row_recv.at[0, 1], sib)]
    for c in meta_out + rows_out:
        c.start()
    for c in loads[2:]:
        c.start()
    start('q', 0, 1)
    for c in loads[:2]:
        c.wait()

    wait('o', 0, 0)
    for c in range(4):
        cols = slice(c * CHUNK, (c + 1) * CHUNK)
        proj = dot(xs[0:tok, :], ring[0, :, cols]).astype(BF16)
        xv[1, 0, :, cols] = (xs[tok:2 * tok, cols].astype(F32) + proj.astype(F32)).astype(BF16)
    start('q', 1, 0)
    u_rows = [remote(xv.at[1, 0], xv.at[1, 2], row_send.at[1, 0], row_recv.at[1, 0], peer),
              remote(xv.at[1, 0], xv.at[1, 1], row_send.at[1, 1], row_recv.at[1, 1], sib)]
    rows_out += u_rows

    def qkv_out(i):
        rows = pl.ds(pl.multiple_of((2 + lax.rem(i, 2)) * tok, tok), tok)
        cols = pl.ds(pl.multiple_of(i * 4 * CHUNK, 4 * CHUNK), 4 * CHUNK)
        return pltpu.make_async_copy(xs.at[rows], qkv_hbm.at[:, cols], out_sem.at[lax.rem(i, 2)])

    def qkv_step(i, carry):
        half = half_at(1 + i)
        wait('q', i, half)

        @pl.when(i >= 2)
        def _():
            qkv_out(i - 2).wait()

        rows = pl.ds(pl.multiple_of((2 + lax.rem(i, 2)) * tok, tok), tok)
        for c in range(4):
            out = dot(xs[tok:2 * tok, :], ring[half, :, c * CHUNK:(c + 1) * CHUNK])
            xs[rows, c * CHUNK:(c + 1) * CHUNK] = out.astype(BF16)

        @pl.when(i + 2 < n_q)
        def _():
            start('q', i + 2, half)

        @pl.when(i + 2 >= n_q)
        def _():
            start('g', i + 2 - n_q, half)

        qkv_out(i).start()

        @pl.when(i == 0)
        def _():
            for c in u_rows:
                c.start()

        return carry

    lax.fori_loop(0, n_q, qkv_step, 0)

    for c in meta_out[:4]:
        c.wait_recv()
    for i, (_, dst, m) in enumerate(meta):
        meta_out.append(remote(dst.at[2, m], dst.at[3, m], meta_send.at[2, i], meta_recv.at[2, i], sib))
        meta_out[-1].start()
    for c in loads[3:]:
        c.wait()
    for c in meta_out[4:]:
        c.wait_recv()
    for c in meta_out:
        c.wait_send()
    first_expert = me * local_n
    expert_rows = lax.broadcasted_iota(jnp.int32, (16, tok), 0)
    before = (lax.broadcasted_iota(jnp.int32, (tok, tok), 0)
              < lax.broadcasted_iota(jnp.int32, (tok, tok), 1)).astype(F32).astype(BF16)
    for k in range(4):
        for m in range(2):
            hit = jnp.zeros((16, tok), F32)
            gate = jnp.zeros((16, tok), F32)
            for c in range(4):
                local = rv[k, m, c:c + 1, :] - first_expert
                same = jnp.broadcast_to(local, (16, tok)) == expert_rows
                hit = jnp.where(same, 1.0, hit)
                gate = jnp.where(same, jnp.broadcast_to(gv[k, m, c:c + 1, :], (16, tok)), gate)
            rank = dot(hit.astype(BF16), before)
            pt[0, m, k] = jnp.where(hit > 0.5, rank + 4.0 * k, -1.0)
            pt[1, m, k] = gate

    def mix_tables(m):
        lanes = gm.shape[3]
        col = lax.broadcasted_iota(jnp.int32, (16, lanes), 1)
        first = WIN * lax.broadcasted_iota(jnp.int32, (16, lanes), 0)
        inside = (col >= first) & (col < first + WIN)
        expand = jnp.where(inside, 1.0, 0.0).astype(BF16)
        offset = jnp.sum(jnp.where(inside, (col - first).astype(F32), 0.0), axis=0, keepdims=True)
        for k in range(4):
            here = dot(pt[0, m, k].T.astype(BF16), expand) == offset
            gate = pt[1, m, k].T
            for i in range(3):
                part = gate.astype(BF16)
                gate = gate - part.astype(F32)
                gm[k, i] = jnp.where(here, dot(part, expand), 0.0).astype(BF16)

    def dispatch(m, k, e0, ne, rows_per, shift):
        rows = lax.broadcasted_iota(jnp.int32, (WIN, tok), 0).astype(F32)
        pick = jnp.concatenate([
            jnp.where(jnp.broadcast_to(pt[0, m, k, e:e + 1, :], (WIN, tok)) == rows, 1.0, 0.0).astype(BF16)
            for e in range(e0, e0 + ne)], axis=0)
        for c in range(0, dim, CHUNK):
            got = dot(pick, xv[m, k, :, c:c + CHUNK]).astype(BF16)
            for e in range(ne):
                lo = e * rows_per + shift + STRIDE * k
                piece = got[e * WIN:(e + 1) * WIN]
                if k == 0:
                    xs[lo:lo + WIN, c:c + CHUNK] = piece
                else:
                    xs[lo:lo + 16, c:c + CHUNK] += piece[:16]
                    xs[lo + 16:lo + WIN, c:c + CHUNK] = piece[16:]

    def expert_hidden(i, half, rows_per, where, refill):
        rows = pl.ds(pl.multiple_of(i * rows_per, 16), rows_per)

        def put(lo, hi, g, u):
            h = (jax.nn.silu(g) * u).astype(BF16)
            for r, shift in enumerate(where):
                hh[i + shift, :, lo:hi] = h[r * SLOTS:(r + 1) * SLOTS]

        for p in range(2):
            g = dot(xs[rows, :], ring[half, :, 2 * p * CHUNK:(2 * p + 1) * CHUNK])
            u = dot(xs[rows, :], ring[half, :, (2 * p + 1) * CHUNK:(2 * p + 2) * CHUNK])
            put(p * CHUNK, (p + 1) * CHUNK, g, u)
            refill((2 * p, 2 * p + 1))
        t = dot(xs[rows, :], ring[half, :, 4 * CHUNK:5 * CHUNK])
        u = dot(xs[rows, :], ring[half, :, 5 * CHUNK:])
        put(1024, 1280, t[:, :256], u)
        put(1280, 1408, t[:, 256:384], t[:, 384:512])
        refill((4, 5))

    def gate_up_a(i, carry):
        half = half_at(base_g + i)
        wait('g', i, half)
        expert_hidden(i, half, SLOTS, (0,), lambda slots: start('g', i + 2, half, slots))
        return carry

    def gate_up_ab(i, carry):
        e = n_first + i
        half = half_at(base_g + e)
        wait('g', e, half)

        def refill(slots):
            if slots[0] == 0:
                return
            ready = range(4) if slots[0] == 2 else range(4, SET)

            @pl.when(e + 2 < local_n)
            def _():
                start('g', e + 2, half, ready)

            @pl.when(e + 2 >= local_n)
            def _():
                start('d', (0, e + 2 - local_n), half, ready)

        expert_hidden(i, half, 2 * SLOTS, (n_first, local_n + n_first), refill)
        return carry

    def mine_out(m, j):
        cols = pl.ds(pl.multiple_of(j * CHUNK, CHUNK), CHUNK)
        return pltpu.make_async_copy(mstage, mine_hbm.at[m, :, cols], mine_sem)

    def back_out(m, j):
        slot = lax.rem(j, 2)
        cols = pl.ds(pl.multiple_of(j * CHUNK, CHUNK), CHUNK)
        return remote(xsend.at[slot], back_hbm.at[m, :, cols], xsend_sem.at[slot], back_sem.at[m, j], peer)

    def sib_out(j):
        slot = lax.rem(j, 2)
        return remote(zs, zr.at[slot], zs_sem, zr_sem.at[slot], sib)

    y_row = n_first * SLOTS
    y_per = local_n - n_first

    def expert_out(m, q, half):
        for c in range(per):
            e = q * per + c
            y = dot(hh[e + m * local_n], ring[half, :ff, c * CHUNK:(c + 1) * CHUNK])
            rows = pl.ds(pl.multiple_of(y_row + lax.rem(e, y_per) * SLOTS, 16), SLOTS)
            cols = pl.ds(pl.multiple_of((e // y_per) * CHUNK, CHUNK), CHUNK)
            xs[rows, cols] = y.astype(BF16)

    def mix(k):
        pieces = []
        for e in range(local_n):
            lo = y_row + (e % y_per) * SLOTS + STRIDE * k
            c = (e // y_per) * CHUNK
            pieces.append(xs[lo:lo + WIN, c:c + CHUNK])
        y = jnp.concatenate(pieces, axis=0)
        return dot(gm[k, 0], y) + dot(gm[k, 1], y) + dot(gm[k, 2], y)

    def to_sibling(m, j):
        if m == 0:
            @pl.when(j >= 1)
            def _():
                sib_out(j - 1).wait_send()
        else:
            sib_out(j + 1).wait_send()
        zs[0] = mix(1)
        zs[1] = mix(3)
        sib_out(j).start()

    def to_peer(m, j):
        slot = lax.rem(j, 2)
        if m == 0:
            @pl.when(j >= 1)
            def _():
                mine_out(0, j - 1).wait()

            @pl.when(j >= 2)
            def _():
                back_out(0, j - 2).wait_send()
        else:
            mine_out(m, j).wait()
            back_out(m, j).wait_send()
        mstage[...] = mix(0)
        xsend[slot] = mix(2)
        sib_out(j).wait_recv()
        xsend[slot] = xsend[slot] + zr[slot, 1]
        back_out(m, j).start()
        mstage[...] = mstage[...] + zr[slot, 0]
        mine_out(m, j).start()

    def down_b(j, carry):
        for q in range(groups):
            half = half_at(base_db + j * groups + q)
            wait('d', (j, q), half)
            expert_out(1, q, half)
            if q + 2 < groups:
                start('d', (j, q + 2), half)
            else:
                @pl.when(j + 1 < n_col)
                def _():
                    start('d', (j + 1, q + 2 - groups), half)
        to_sibling(1, j)
        to_peer(1, j)
        return carry

    def down_a_gate_b(t, carry):
        first = base_mix + t * (groups + each)
        for q in range(groups):
            half = half_at(first + q)
            wait('d', (t, q), half)
            expert_out(0, q, half)
            if q + 2 < groups:
                start('d', (t, q + 2), half)
            else:
                start('g', t * each + q + 2 - groups, half)
        to_sibling(0, t)

        @pl.when(t == 0)
        def _():
            for k in range(4):
                dispatch(1, k, 0, n_first, SLOTS, 0)

        for r in range(each):
            half = half_at(first + groups + r)
            e = t * each + r
            wait('g', e, half)
            expert_hidden(e, half, SLOTS, (local_n,), lambda slots: start('d', (lax.rem(t + 1, n_col), r), half, slots))
            if r == 0:
                to_peer(0, t)

                @pl.when(t == n_col - 1)
                def _():
                    mix_tables(1)

        return carry

    def forward(m):
        rows_out[2 * m].wait_recv()
        c = remote(xv.at[m, 2], xv.at[m, 3], row_send.at[m, 2], row_recv.at[m, 2], sib)
        c.start()
        return c

    for i in (n_q - 2, n_q - 1):
        qkv_out(i).wait()
    loads[2].wait()
    rows_out[1].wait_recv()
    dispatch(0, 0, 0, n_first, SLOTS, 0)
    dispatch(0, 1, 0, n_first, SLOTS, 0)
    forward_a = forward(0)
    dispatch(0, 2, 0, n_first, SLOTS, 0)
    forward_a.wait_recv()
    dispatch(0, 3, 0, n_first, SLOTS, 0)
    lax.fori_loop(0, n_first, gate_up_a, 0)
    for k in range(4):
        dispatch(0, k, n_first, n_both, 2 * SLOTS, 0)
    rows_out[3].wait_recv()
    dispatch(1, 0, n_first, n_both, 2 * SLOTS, SLOTS)
    dispatch(1, 1, n_first, n_both, 2 * SLOTS, SLOTS)
    forward_b = forward(1)
    dispatch(1, 2, n_first, n_both, 2 * SLOTS, SLOTS)
    mix_tables(0)
    forward_b.wait_recv()
    dispatch(1, 3, n_first, n_both, 2 * SLOTS, SLOTS)
    lax.fori_loop(0, n_both, gate_up_ab, 0)
    lax.fori_loop(0, n_col, down_a_gate_b, 0)
    lax.fori_loop(0, n_col, down_b, 0)

    sib_out(n_col - 1).wait_send()
    mine_out(1, n_col - 1).wait()
    for j in (n_col - 2, n_col - 1):
        back_out(1, j).wait_send()
    outs = []
    for m in range(2):
        for j in range(n_col):
            slot = j % 2
            cols = slice(j * CHUNK, (j + 1) * CHUNK)
            back_out(m, j).wait_recv()
            parts = [
                pltpu.make_async_copy(mine_hbm.at[m, :, cols], zr.at[slot, 0], final_sem.at[0]),
                pltpu.make_async_copy(back_hbm.at[m, :, cols], zr.at[slot, 1], final_sem.at[1]),
            ]
            for c in parts:
                c.start()
            for c in parts:
                c.wait()
            total_row = xv[m, 0, :, cols].astype(F32) + (zr[slot, 0] + zr[slot, 1])
            xs[m * tok:(m + 1) * tok, cols] = total_row.astype(BF16)
            out = pltpu.make_async_copy(
                xs.at[m * tok:(m + 1) * tok, cols], (outa_hbm, outb_hbm)[m].at[:, cols], last_sem.at[m, j])
            out.start()
            outs.append(out)
    for c in rows_out + [forward_a, forward_b]:
        c.wait_send()
    for c in outs:
        c.wait()


def moe_layer(x_a, h_b, attn_b, r_a, r_b, g_a, g_b, w_qkv, w_o, w_gate, w_up, w_down):
    tok, dim = x_a.shape
    local_n, ff, _ = w_down.shape
    hbm = pl.BlockSpec(memory_space=pl.ANY)
    dma = pltpu.SemaphoreType.DMA
    flops = 2 * tok * dim * (dim + w_qkv.shape[1]) + local_n * 2 * SLOTS * 6 * dim * ff
    return pl.pallas_call(
        layer_kernel,
        in_specs=[hbm] * 12,
        out_specs=[hbm] * 5,
        out_shape=[
            jax.ShapeDtypeStruct((2, tok, dim), F32),
            jax.ShapeDtypeStruct((2, tok, dim), F32),
            jax.ShapeDtypeStruct((tok, dim), BF16),
            jax.ShapeDtypeStruct((tok, dim), BF16),
            jax.ShapeDtypeStruct((tok, w_qkv.shape[1]), BF16),
        ],
        scratch_shapes=[
            pltpu.VMEM((2, 4, tok, dim), BF16),
            pltpu.VMEM((local_n * SLOTS, dim), BF16),
            pltpu.VMEM((2 * local_n, SLOTS, ff), BF16),
            pltpu.VMEM((2, dim, 5 * CHUNK + 256), BF16),
            pltpu.VMEM((4, 3, tok, local_n * WIN), BF16),
            pltpu.VMEM((4, 2, 4, tok), jnp.int32),
            pltpu.VMEM((4, 2, 4, tok), F32),
            pltpu.VMEM((2, 2, 4, 16, tok), F32),
            pltpu.VMEM((2, tok, CHUNK), F32),
            pltpu.VMEM((2, 2, tok, CHUNK), F32),
            pltpu.VMEM((2, tok, CHUNK), F32),
            pltpu.VMEM((tok, CHUNK), F32),
            dma((2, SET)), dma((2,)), dma((7,)), dma((2,)), dma((3, 4)), dma((3, 4)), dma((2, 3)), dma((2, 3)),
            dma(()), dma((2,)), dma((2,)), dma((2, dim // CHUNK)), dma(()), dma((2, dim // CHUNK)), dma((2,)),
        ],
        compiler_params=pltpu.CompilerParams(
            collective_id=0, has_side_effects=True, vmem_limit_bytes=VMEM_LIMIT),
        cost_estimate=pl.CostEstimate(flops=flops, bytes_accessed=local_n * 6 * dim * ff, transcendentals=0),
        name='moe_layer',
    )(x_a, h_b, attn_b, r_a, r_b, g_a, g_b, w_qkv, w_o, w_gate, w_up, w_down)


def hand_on_kernel(n, *refs):
    ins, outs, bufs = refs[:n], refs[n:2 * n], refs[2 * n:3 * n]
    in_sem, out_sem = refs[3 * n:]
    parts = []
    for a in range(n):
        for p in range(ins[a].shape[1] // 1024):
            parts.append((a, slice(1024 * p, 1024 * (p + 1)), len(parts)))
    gets = [pltpu.make_async_copy(ins[a].at[:, c], bufs[a].at[:, c], in_sem.at[i]) for a, c, i in parts]
    puts = [pltpu.make_async_copy(bufs[a].at[:, c], outs[a].at[:, c], out_sem.at[i]) for a, c, i in parts]
    for g in gets:
        g.start()
    for g, p in zip(gets, puts):
        g.wait()
        p.start()
    for p in puts:
        p.wait()


def hand_on(*arrays):
    n = len(arrays)
    count = sum(a.shape[1] // 1024 for a in arrays)
    hbm = pl.BlockSpec(memory_space=pl.ANY)
    return pl.pallas_call(
        functools.partial(hand_on_kernel, n),
        in_specs=[hbm] * n,
        out_specs=[hbm] * n,
        out_shape=[jax.ShapeDtypeStruct(a.shape, a.dtype) for a in arrays],
        scratch_shapes=[pltpu.VMEM(a.shape, a.dtype) for a in arrays] + [
            pltpu.SemaphoreType.DMA((count,)), pltpu.SemaphoreType.DMA((count,))],
        compiler_params=pltpu.CompilerParams(vmem_limit_bytes=VMEM_LIMIT),
        name='hand_on',
    )(*arrays)


def solution(mesh):
    def local_step(x_a, route_a, gate_a, h_b, attn_b, route_b, gate_b, w_qkv, w_o, w_gate, w_up, w_down):
        _, _, out_a, out_b, qkv_b = moe_layer(
            x_a, h_b, attn_b, route_a.T, route_b.T, gate_a.T, gate_b.T, w_qkv, w_o, w_gate, w_up, w_down)
        out_a, out_b, qkv_b = hand_on(out_a, out_b, qkv_b)
        return out_a, out_b, qkv_b

    row_spec = P(('dp', 'ep'), None)
    full_spec = P(None, None)
    expert_spec = P('ep', None, None)
    return jax.shard_map(
        local_step,
        mesh=mesh,
        in_specs=(row_spec, row_spec, row_spec, row_spec, row_spec, row_spec, row_spec, full_spec, full_spec, expert_spec, expert_spec, expert_spec),
        out_specs=(row_spec, row_spec, row_spec),
        check_vma=False,
    )
```

time: 229 us -> 216 us (0.943)
  local copies, waits for them, and re-layouts: 8.49 us -> 0 us
  Pallas kernels: 217 us -> 214 us
    unnamed x3 -> x0, local copies, waits for them, and re-layouts: 8.49 us -> none
    pallas_call x1 -> x2, Pallas kernels: 217 us -> 214 us  [the longest x1 210 us: moe_layer(): pl.pallas_call(layer_kernel, in_specs=[hbm] * 12, out_specs=[hbm] * 5, ou...]
where the time goes in v4:
time: 216 us; the launch traced here: 215 us
  Pallas kernels  214 us (99%)
    pallas_call x1, Pallas kernels, moe_layer(): pl.pallas_call(layer_kernel, in_specs=[hbm] * 12, out_specs=[hbm] * 5, ou...  210 us
    pallas_call x1, Pallas kernels, hand_on(): pl.pallas_call(functools.partial(hand_on_kernel, n), in_specs=[hbm] * n,...  4.77 us

profile of v4, /device:TPU:0, one launch (start us, length us, event | category | flops | bytes accessed | tf_op | source)
XLA Modules:
  0.0 215.3 jit_solution(10561066117529492031)
XLA Ops:
  0.6 209.7 %moe_layer.1 = (f32[2,256,2048]{2,1,0:T(8,128)}, f32[2,256,2048]{2,1,0:T(8,128)}, bf16[256,2048]{1,0:T(8,128)(2,1)}, bf16[256,2048]{1,0:T(8,128)(2,1)}, bf16[256,6144]{1,0:T(8,128)(2,1)}) custom-call(bf16[256,2048]{1,0:T(8,128)(2,1)} %x_hbm.1, bf16[256,2048]{1,0:T(8,128)(2,1)} %h_hbm.1, bf16[256,2048]{1,0:T(8,128)(2,1)} %attn_hbm.1, s32[4,256]{1,0:T(4,128)} %bitcast.4, ...), custom_call_target="tpu_custom_call" | custom-call | flops 83332431872 | bytes 259522560 | tf_op jit(solution)/shard_map/moe_layer/pallas_call | solution.py:452
  210.3 4.8 %hand_on.1 = (bf16[256,2048]{1,0:T(8,128)(2,1)}, bf16[256,2048]{1,0:T(8,128)(2,1)}, bf16[256,6144]{1,0:T(8,128)(2,1)}) custom-call(bf16[256,2048]{1,0:T(8,128)(2,1)} %get-tuple-element.6.refs_0_, bf16[256,2048]{1,0:T(8,128)(2,1)} %get-tuple-element.7.refs_1_, bf16[256,6144]{1,0:T(8,128)(2,1)} %get-tuple-element.8.refs_2_), custom_call_target="tpu_custom_call" | custom-call | tf_op jit(solution)/shard_map/hand_on/pallas_call | solution.py:508

commit v5 on v4

--- a/solution.py
+++ b/solution.py
@@ -24,14 +24,14 @@
 
 def layer_kernel(
     x_hbm, h_hbm, attn_hbm, ra_hbm, rb_hbm, ga_hbm, gb_hbm, wqkv_hbm, wo_hbm, wg_hbm, wu_hbm, wd_hbm,
-    mine_hbm, back_hbm, outa_hbm, outb_hbm, qkv_hbm,
+    mine_hbm, back_hbm, outa_hbm, outb_hbm, qkv_hbm, table_hbm,
     xv, xs, hh, ring, gm, rv, gv, pt, zs, zr, xsend, mstage,
     ring_sem, tail_sem, load_sem, out_sem, meta_send, meta_recv, row_send, row_recv,
-    zs_sem, zr_sem, xsend_sem, back_sem, mine_sem, last_sem, final_sem,
+    zs_sem, zr_sem, xsend_sem, back_sem, mine_sem, last_sem, final_sem, table_sem,
 ):
     tok, dim = x_hbm.shape
     local_n, ff, _ = wd_hbm.shape
-    n_first = (local_n + 1) // 2
+    n_first = local_n // 2
     n_both = local_n - n_first
     per = 5
     n_col = dim // CHUNK
@@ -45,7 +45,7 @@
             src_ref=src, dst_ref=dst, send_sem=send, recv_sem=recv, device_id=who, device_id_type=mesh_id)
 
     groups = local_n // per
-    each = n_first // n_col
+    each = (n_first + n_col - 1) // n_col
     n_q = wqkv_hbm.shape[1] // (4 * CHUNK)
     base_g = 1 + n_q
     base_mix = base_g + local_n
@@ -194,20 +194,25 @@
             pt[0, m, k] = jnp.where(hit > 0.5, rank + 4.0 * k, -1.0)
             pt[1, m, k] = gate
 
-    def mix_tables(m):
+    def mix_table(m, k):
         lanes = gm.shape[3]
         col = lax.broadcasted_iota(jnp.int32, (16, lanes), 1)
         first = WIN * lax.broadcasted_iota(jnp.int32, (16, lanes), 0)
         inside = (col >= first) & (col < first + WIN)
         expand = jnp.where(inside, 1.0, 0.0).astype(BF16)
         offset = jnp.sum(jnp.where(inside, (col - first).astype(F32), 0.0), axis=0, keepdims=True)
-        for k in range(4):
-            here = dot(pt[0, m, k].T.astype(BF16), expand) == offset
-            gate = pt[1, m, k].T
-            for i in range(3):
-                part = gate.astype(BF16)
-                gate = gate - part.astype(F32)
-                gm[k, i] = jnp.where(here, dot(part, expand), 0.0).astype(BF16)
+        here = dot(pt[0, m, k].T.astype(BF16), expand) == offset
+        gate = pt[1, m, k].T
+        for i in range(3):
+            part = gate.astype(BF16)
+            gate = gate - part.astype(F32)
+            gm[k, i] = jnp.where(here, dot(part, expand), 0.0).astype(BF16)
+
+    def table_out(k):
+        return pltpu.make_async_copy(gm.at[k], table_hbm.at[k], table_sem.at[k])
+
+    def table_back(k):
+        return pltpu.make_async_copy(table_hbm.at[k], gm.at[k], table_sem.at[k])
 
     def dispatch(m, k, e0, ne, rows_per, shift):
         rows = lax.broadcasted_iota(jnp.int32, (WIN, tok), 0).astype(F32)
@@ -248,6 +253,17 @@
         half = half_at(base_g + i)
         wait('g', i, half)
         expert_hidden(i, half, SLOTS, (0,), lambda slots: start('g', i + 2, half, slots))
+
+        @pl.when(i < 4)
+        def _():
+            mix_table(1, i)
+            table_out(i).start()
+
+        @pl.when((i >= 3) & (i < 7))
+        def _():
+            table_out(i - 3).wait()
+            mix_table(0, i - 3)
+
         return carry
 
     def gate_up_ab(i, carry):
@@ -347,6 +363,12 @@
                 @pl.when(j + 1 < n_col)
                 def _():
                     start('d', (j + 1, q + 2 - groups), half)
+
+        @pl.when(j == 0)
+        def _():
+            for k in range(4):
+                table_back(k).wait()
+
         to_sibling(1, j)
         to_peer(1, j)
         return carry
@@ -359,26 +381,48 @@
             expert_out(0, q, half)
             if q + 2 < groups:
                 start('d', (t, q + 2), half)
+            elif q + 2 == groups:
+                start('g', t * each, half)
             else:
-                start('g', t * each + q + 2 - groups, half)
+                @pl.when(t * each + 1 < n_first)
+                def _():
+                    start('g', t * each + 1, half)
+
+                @pl.when(t * each + 1 >= n_first)
+                def _():
+                    start('d', (0, 0), half)
         to_sibling(0, t)
+
+        @pl.when(t == n_col - 1)
+        def _():
+            table_back(1).start()
+            table_back(3).start()
 
         @pl.when(t == 0)
         def _():
             for k in range(4):
                 dispatch(1, k, 0, n_first, SLOTS, 0)
 
-        for r in range(each):
+        to_peer(0, t)
+
+        @pl.when(t == n_col - 1)
+        def _():
+            table_back(0).start()
+            table_back(2).start()
+
+        def hidden(r):
             half = half_at(first + groups + r)
             e = t * each + r
+            ahead = r + lax.div(t + 1, n_col)
             wait('g', e, half)
-            expert_hidden(e, half, SLOTS, (local_n,), lambda slots: start('d', (lax.rem(t + 1, n_col), r), half, slots))
-            if r == 0:
-                to_peer(0, t)
-
-                @pl.when(t == n_col - 1)
-                def _():
-                    mix_tables(1)
+            expert_hidden(
+                e, half, SLOTS, (local_n,), lambda slots: start('d', (lax.rem(t + 1, n_col), ahead), half, slots))
+
+        hidden(0)
+
+        @pl.when(t * each + 1 < n_first)
+        def _():
+            hidden(1)
 
         return carry
 
@@ -406,7 +450,6 @@
     dispatch(1, 1, n_first, n_both, 2 * SLOTS, SLOTS)
     forward_b = forward(1)
     dispatch(1, 2, n_first, n_both, 2 * SLOTS, SLOTS)
-    mix_tables(0)
     forward_b.wait_recv()
     dispatch(1, 3, n_first, n_both, 2 * SLOTS, SLOTS)
     lax.fori_loop(0, n_both, gate_up_ab, 0)
@@ -415,8 +458,6 @@
 
     sib_out(n_col - 1).wait_send()
     mine_out(1, n_col - 1).wait()
-    for j in (n_col - 2, n_col - 1):
-        back_out(1, j).wait_send()
     outs = []
     for m in range(2):
         for j in range(n_col):
@@ -437,6 +478,8 @@
                 xs.at[m * tok:(m + 1) * tok, cols], (outa_hbm, outb_hbm)[m].at[:, cols], last_sem.at[m, j])
             out.start()
             outs.append(out)
+    for j in (n_col - 2, n_col - 1):
+        back_out(1, j).wait_send()
     for c in rows_out + [forward_a, forward_b]:
         c.wait_send()
     for c in outs:
@@ -452,17 +495,18 @@
     return pl.pallas_call(
         layer_kernel,
         in_specs=[hbm] * 12,
-        out_specs=[hbm] * 5,
+        out_specs=[hbm] * 6,
         out_shape=[
             jax.ShapeDtypeStruct((2, tok, dim), F32),
             jax.ShapeDtypeStruct((2, tok, dim), F32),
             jax.ShapeDtypeStruct((tok, dim), BF16),
             jax.ShapeDtypeStruct((tok, dim), BF16),
             jax.ShapeDtypeStruct((tok, w_qkv.shape[1]), BF16),
+            jax.ShapeDtypeStruct((4, 3, tok, local_n * WIN), BF16),
         ],
         scratch_shapes=[
             pltpu.VMEM((2, 4, tok, dim), BF16),
-            pltpu.VMEM((local_n * SLOTS, dim), BF16),
+            pltpu.VMEM(((local_n + local_n % 2) * SLOTS, dim), BF16),
             pltpu.VMEM((2 * local_n, SLOTS, ff), BF16),
             pltpu.VMEM((2, dim, 5 * CHUNK + 256), BF16),
             pltpu.VMEM((4, 3, tok, local_n * WIN), BF16),
@@ -474,7 +518,7 @@
             pltpu.VMEM((2, tok, CHUNK), F32),
             pltpu.VMEM((tok, CHUNK), F32),
             dma((2, SET)), dma((2,)), dma((7,)), dma((2,)), dma((3, 4)), dma((3, 4)), dma((2, 3)), dma((2, 3)),
-            dma(()), dma((2,)), dma((2,)), dma((2, dim // CHUNK)), dma(()), dma((2, dim // CHUNK)), dma((2,)),
+            dma(()), dma((2,)), dma((2,)), dma((2, dim // CHUNK)), dma(()), dma((2, dim // CHUNK)), dma((2,)), dma((4,)),
         ],
         compiler_params=pltpu.CompilerParams(
             collective_id=0, has_side_effects=True, vmem_limit_bytes=VMEM_LIMIT),
@@ -519,7 +563,7 @@
 
 def solution(mesh):
     def local_step(x_a, route_a, gate_a, h_b, attn_b, route_b, gate_b, w_qkv, w_o, w_gate, w_up, w_down):
-        _, _, out_a, out_b, qkv_b = moe_layer(
+        _, _, out_a, out_b, qkv_b, _ = moe_layer(
             x_a, h_b, attn_b, route_a.T, route_b.T, gate_a.T, gate_b.T, w_qkv, w_o, w_gate, w_up, w_down)
         out_a, out_b, qkv_b = hand_on(out_a, out_b, qkv_b)
         return out_a, out_b, qkv_b

time: 216 us -> 208 us (0.963)
  Pallas kernels: 214 us -> 207 us
    pallas_call x1, Pallas kernels: 210 us -> 202 us  [moe_layer(): pl.pallas_call(layer_kernel, in_specs=[hbm] * 12, out_specs=[hbm] * 6, ou...]
where the time goes in v5:
time: 208 us; the launch traced here: 207 us
  Pallas kernels  207 us (100%)
    pallas_call x1, Pallas kernels, moe_layer(): pl.pallas_call(layer_kernel, in_specs=[hbm] * 12, out_specs=[hbm] * 6, ou...  202 us
    pallas_call x1, Pallas kernels, hand_on(): pl.pallas_call(functools.partial(hand_on_kernel, n), in_specs=[hbm] * n,...  4.77 us

profile of v5, /device:TPU:0, one launch (start us, length us, event | category | flops | bytes accessed | tf_op | source)
XLA Modules:
  0.0 207.4 jit_solution(14294301105635820555)
XLA Ops:
  0.6 201.9 %moe_layer.1 = (f32[2,256,2048]{2,1,0:T(8,128)}, f32[2,256,2048]{2,1,0:T(8,128)}, bf16[256,2048]{1,0:T(8,128)(2,1)}, bf16[256,2048]{1,0:T(8,128)(2,1)}, bf16[256...) custom-call(bf16[256,2048]{1,0:T(8,128)(2,1)} %x_hbm.1, bf16[256,2048]{1,0:T(8,128)(2,1)} %h_hbm.1, ...), custom_call_target="tpu_custom_call" | custom-call | flops 83332431872 | bytes 259522560 | tf_op jit(solution)/shard_map/moe_layer/pallas_call | solution.py:495
  202.5 4.8 %hand_on.1 = (bf16[256,2048]{1,0:T(8,128)(2,1)}, bf16[256,2048]{1,0:T(8,128)(2,1)}, bf16[256,6144]{1,0:T(8,128)(2,1)}) custom-call(bf16[256,2048]{1,0:T(8,128)(2,1)} %get-tuple-element.6.refs_0_, bf16[256,2048]{1,0:T(8,128)(2,1)} %get-tuple-element.7.refs_1_, bf16[256,6144]{1,0:T(8,128)(2,1)} %get-tuple-element.8.refs_2_), custom_call_target="tpu_custom_call" | custom-call | tf_op jit(solution)/shard_map/hand_on/pallas_call | solution.py:552

commit v6 on v5

--- a/solution.py
+++ b/solution.py
@@ -27,7 +27,7 @@
     mine_hbm, back_hbm, outa_hbm, outb_hbm, qkv_hbm, table_hbm,
     xv, xs, hh, ring, gm, rv, gv, pt, zs, zr, xsend, mstage,
     ring_sem, tail_sem, load_sem, out_sem, meta_send, meta_recv, row_send, row_recv,
-    zs_sem, zr_sem, xsend_sem, back_sem, mine_sem, last_sem, final_sem, table_sem,
+    zs_sem, zr_sem, xsend_sem, back_sem, mine_sem, last_sem, final_sem, table_sem, early_sem,
 ):
     tok, dim = x_hbm.shape
     local_n, ff, _ = wd_hbm.shape
@@ -48,7 +48,7 @@
     each = (n_first + n_col - 1) // n_col
     n_q = wqkv_hbm.shape[1] // (4 * CHUNK)
     base_g = 1 + n_q
-    base_mix = base_g + local_n
+    base_mix = base_g + local_n - 1
     base_db = base_mix + n_col * groups + n_first
 
     def half_at(it):
@@ -153,7 +153,7 @@
 
         @pl.when(i + 2 >= n_q)
         def _():
-            start('g', i + 2 - n_q, half)
+            start('g', i + 3 - n_q, half)
 
         qkv_out(i).start()
 
@@ -165,6 +165,10 @@
         return carry
 
     lax.fori_loop(0, n_q, qkv_step, 0)
+    early = [pltpu.make_async_copy(wg_hbm.at[0], hh.at[0:dim], early_sem.at[0]),
+             pltpu.make_async_copy(wu_hbm.at[0], hh.at[dim:2 * dim], early_sem.at[1])]
+    for c in early:
+        c.start()
 
     for c in meta_out[:4]:
         c.wait_recv()
@@ -230,13 +234,30 @@
                     xs[lo:lo + 16, c:c + CHUNK] += piece[:16]
                     xs[lo + 16:lo + WIN, c:c + CHUNK] = piece[16:]
 
+    def hidden_rows(i):
+        return pl.ds(pl.multiple_of(i * SLOTS, 16), SLOTS)
+
+    def first_hidden():
+        for c in early:
+            c.wait()
+        x = slice(0, SLOTS)
+        spare = slice(n_first * SLOTS, (n_first + 1) * SLOTS)
+        for lo in range(0, ff, CHUNK):
+            hi = min(lo + CHUNK, ff)
+            g = dot(xs[x, :], hh[0:dim, lo:hi])
+            u = dot(xs[x, :], hh[dim:2 * dim, lo:hi])
+            xs[spare, lo:hi] = (jax.nn.silu(g) * u).astype(BF16)
+        hh[0:SLOTS, :] = xs[spare, 0:ff]
+        mix_table(1, 0)
+        table_out(0).start()
+
     def expert_hidden(i, half, rows_per, where, refill):
         rows = pl.ds(pl.multiple_of(i * rows_per, 16), rows_per)
 
         def put(lo, hi, g, u):
             h = (jax.nn.silu(g) * u).astype(BF16)
             for r, shift in enumerate(where):
-                hh[i + shift, :, lo:hi] = h[r * SLOTS:(r + 1) * SLOTS]
+                hh[hidden_rows(i + shift), lo:hi] = h[r * SLOTS:(r + 1) * SLOTS]
 
         for p in range(2):
             g = dot(xs[rows, :], ring[half, :, 2 * p * CHUNK:(2 * p + 1) * CHUNK])
@@ -250,7 +271,7 @@
         refill((4, 5))
 
     def gate_up_a(i, carry):
-        half = half_at(base_g + i)
+        half = half_at(base_g + i - 1)
         wait('g', i, half)
         expert_hidden(i, half, SLOTS, (0,), lambda slots: start('g', i + 2, half, slots))
 
@@ -268,7 +289,7 @@
 
     def gate_up_ab(i, carry):
         e = n_first + i
-        half = half_at(base_g + e)
+        half = half_at(base_g + e - 1)
         wait('g', e, half)
 
         def refill(slots):
@@ -306,7 +327,7 @@
     def expert_out(m, q, half):
         for c in range(per):
             e = q * per + c
-            y = dot(hh[e + m * local_n], ring[half, :ff, c * CHUNK:(c + 1) * CHUNK])
+            y = dot(hh[hidden_rows(e + m * local_n), :], ring[half, :ff, c * CHUNK:(c + 1) * CHUNK])
             rows = pl.ds(pl.multiple_of(y_row + lax.rem(e, y_per) * SLOTS, 16), SLOTS)
             cols = pl.ds(pl.multiple_of((e // y_per) * CHUNK, CHUNK), CHUNK)
             xs[rows, cols] = y.astype(BF16)
@@ -442,7 +463,8 @@
     dispatch(0, 2, 0, n_first, SLOTS, 0)
     forward_a.wait_recv()
     dispatch(0, 3, 0, n_first, SLOTS, 0)
-    lax.fori_loop(0, n_first, gate_up_a, 0)
+    first_hidden()
+    lax.fori_loop(1, n_first, gate_up_a, 0)
     for k in range(4):
         dispatch(0, k, n_first, n_both, 2 * SLOTS, 0)
     rows_out[3].wait_recv()
@@ -507,7 +529,7 @@
         scratch_shapes=[
             pltpu.VMEM((2, 4, tok, dim), BF16),
             pltpu.VMEM(((local_n + local_n % 2) * SLOTS, dim), BF16),
-            pltpu.VMEM((2 * local_n, SLOTS, ff), BF16),
+            pltpu.VMEM((2 * local_n * SLOTS, ff), BF16),
             pltpu.VMEM((2, dim, 5 * CHUNK + 256), BF16),
             pltpu.VMEM((4, 3, tok, local_n * WIN), BF16),
             pltpu.VMEM((4, 2, 4, tok), jnp.int32),
@@ -518,7 +540,7 @@
             pltpu.VMEM((2, tok, CHUNK), F32),
             pltpu.VMEM((tok, CHUNK), F32),
             dma((2, SET)), dma((2,)), dma((7,)), dma((2,)), dma((3, 4)), dma((3, 4)), dma((2, 3)), dma((2, 3)),
-            dma(()), dma((2,)), dma((2,)), dma((2, dim // CHUNK)), dma(()), dma((2, dim // CHUNK)), dma((2,)), dma((4,)),
+            dma(()), dma((2,)), dma((2,)), dma((2, dim // CHUNK)), dma(()), dma((2, dim // CHUNK)), dma((2,)), dma((4,)), dma((2,)),
         ],
         compiler_params=pltpu.CompilerParams(
             collective_id=0, has_side_effects=True, vmem_limit_bytes=VMEM_LIMIT),

time: 208 us -> 207 us (level)
  no operation moved by 1% of the time
where the time goes in v6:
time: 207 us; the launch traced here: 206 us
  Pallas kernels  206 us (100%)
    pallas_call x1, Pallas kernels, moe_layer(): pl.pallas_call(layer_kernel, in_specs=[hbm] * 12, out_specs=[hbm] * 6, ou...  201 us
    pallas_call x1, Pallas kernels, hand_on(): pl.pallas_call(functools.partial(hand_on_kernel, n), in_specs=[hbm] * n,...  4.77 us

profile of v6, /device:TPU:0, one launch (start us, length us, event | category | flops | bytes accessed | tf_op | source)
XLA Modules:
  0.0 206.4 jit_solution(11567182329817450264)
XLA Ops:
  0.6 200.8 %moe_layer.1 = (f32[2,256,2048]{2,1,0:T(8,128)}, f32[2,256,2048]{2,1,0:T(8,128)}, bf16[256,2048]{1,0:T(8,128)(2,1)}, bf16[256,2048]{1,0:T(8,128)(2,1)}, bf16[256...) custom-call(bf16[256,2048]{1,0:T(8,128)(2,1)} %x_hbm.1, bf16[256,2048]{1,0:T(8,128)(2,1)} %h_hbm.1, ...), custom_call_target="tpu_custom_call" | custom-call | flops 83332431872 | bytes 259522560 | tf_op jit(solution)/shard_map/moe_layer/pallas_call | solution.py:517
  201.4 4.8 %hand_on.1 = (bf16[256,2048]{1,0:T(8,128)(2,1)}, bf16[256,2048]{1,0:T(8,128)(2,1)}, bf16[256,6144]{1,0:T(8,128)(2,1)}) custom-call(bf16[256,2048]{1,0:T(8,128)(2,1)} %get-tuple-element.6.refs_0_, bf16[256,2048]{1,0:T(8,128)(2,1)} %get-tuple-element.7.refs_1_, bf16[256,6144]{1,0:T(8,128)(2,1)} %get-tuple-element.8.refs_2_), custom_call_target="tpu_custom_call" | custom-call | tf_op jit(solution)/shard_map/hand_on/pallas_call | solution.py:574

commit v7 on v6

--- a/solution.py
+++ b/solution.py
@@ -24,10 +24,10 @@
 
 def layer_kernel(
     x_hbm, h_hbm, attn_hbm, ra_hbm, rb_hbm, ga_hbm, gb_hbm, wqkv_hbm, wo_hbm, wg_hbm, wu_hbm, wd_hbm,
-    mine_hbm, back_hbm, outa_hbm, outb_hbm, qkv_hbm, table_hbm,
+    mine_hbm, back_hbm, outa_hbm, outb_hbm, qkv_hbm,
     xv, xs, hh, ring, gm, rv, gv, pt, zs, zr, xsend, mstage,
     ring_sem, tail_sem, load_sem, out_sem, meta_send, meta_recv, row_send, row_recv,
-    zs_sem, zr_sem, xsend_sem, back_sem, mine_sem, last_sem, final_sem, table_sem, early_sem,
+    zs_sem, zr_sem, xsend_sem, back_sem, mine_sem, last_sem, final_sem, early_sem,
 ):
     tok, dim = x_hbm.shape
     local_n, ff, _ = wd_hbm.shape
@@ -212,12 +212,6 @@
             gate = gate - part.astype(F32)
             gm[k, i] = jnp.where(here, dot(part, expand), 0.0).astype(BF16)
 
-    def table_out(k):
-        return pltpu.make_async_copy(gm.at[k], table_hbm.at[k], table_sem.at[k])
-
-    def table_back(k):
-        return pltpu.make_async_copy(table_hbm.at[k], gm.at[k], table_sem.at[k])
-
     def dispatch(m, k, e0, ne, rows_per, shift):
         rows = lax.broadcasted_iota(jnp.int32, (WIN, tok), 0).astype(F32)
         pick = jnp.concatenate([
@@ -248,8 +242,6 @@
             u = dot(xs[x, :], hh[dim:2 * dim, lo:hi])
             xs[spare, lo:hi] = (jax.nn.silu(g) * u).astype(BF16)
         hh[0:SLOTS, :] = xs[spare, 0:ff]
-        mix_table(1, 0)
-        table_out(0).start()
 
     def expert_hidden(i, half, rows_per, where, refill):
         rows = pl.ds(pl.multiple_of(i * rows_per, 16), rows_per)
@@ -275,15 +267,9 @@
         wait('g', i, half)
         expert_hidden(i, half, SLOTS, (0,), lambda slots: start('g', i + 2, half, slots))
 
-        @pl.when(i < 4)
-        def _():
-            mix_table(1, i)
-            table_out(i).start()
-
-        @pl.when((i >= 3) & (i < 7))
-        def _():
-            table_out(i - 3).wait()
-            mix_table(0, i - 3)
+        @pl.when(i <= 4)
+        def _():
+            mix_table(0, i - 1)
 
         return carry
 
@@ -384,11 +370,6 @@
                 @pl.when(j + 1 < n_col)
                 def _():
                     start('d', (j + 1, q + 2 - groups), half)
-
-        @pl.when(j == 0)
-        def _():
-            for k in range(4):
-                table_back(k).wait()
 
         to_sibling(1, j)
         to_peer(1, j)
@@ -416,8 +397,8 @@
 
         @pl.when(t == n_col - 1)
         def _():
-            table_back(1).start()
-            table_back(3).start()
+            mix_table(1, 1)
+            mix_table(1, 3)
 
         @pl.when(t == 0)
         def _():
@@ -428,8 +409,8 @@
 
         @pl.when(t == n_col - 1)
         def _():
-            table_back(0).start()
-            table_back(2).start()
+            mix_table(1, 0)
+            mix_table(1, 2)
 
         def hidden(r):
             half = half_at(first + groups + r)
@@ -485,6 +466,12 @@
         for j in range(n_col):
             slot = j % 2
             cols = slice(j * CHUNK, (j + 1) * CHUNK)
+            if (m, j) == (1, n_col - 1):
+                out = pltpu.make_async_copy(xv.at[m, 0, :, cols], outb_hbm.at[:, cols], last_sem.at[m, j])
+                out.start()
+                outs.append(out)
+                back_out(m, j).wait_recv()
+                continue
             back_out(m, j).wait_recv()
             parts = [
                 pltpu.make_async_copy(mine_hbm.at[m, :, cols], zr.at[slot, 0], final_sem.at[0]),
@@ -517,14 +504,13 @@
     return pl.pallas_call(
         layer_kernel,
         in_specs=[hbm] * 12,
-        out_specs=[hbm] * 6,
+        out_specs=[hbm] * 5,
         out_shape=[
             jax.ShapeDtypeStruct((2, tok, dim), F32),
             jax.ShapeDtypeStruct((2, tok, dim), F32),
             jax.ShapeDtypeStruct((tok, dim), BF16),
             jax.ShapeDtypeStruct((tok, dim), BF16),
             jax.ShapeDtypeStruct((tok, w_qkv.shape[1]), BF16),
-            jax.ShapeDtypeStruct((4, 3, tok, local_n * WIN), BF16),
         ],
         scratch_shapes=[
             pltpu.VMEM((2, 4, tok, dim), BF16),
@@ -540,7 +526,7 @@
             pltpu.VMEM((2, tok, CHUNK), F32),
             pltpu.VMEM((tok, CHUNK), F32),
             dma((2, SET)), dma((2,)), dma((7,)), dma((2,)), dma((3, 4)), dma((3, 4)), dma((2, 3)), dma((2, 3)),
-            dma(()), dma((2,)), dma((2,)), dma((2, dim // CHUNK)), dma(()), dma((2, dim // CHUNK)), dma((2,)), dma((4,)), dma((2,)),
+            dma(()), dma((2,)), dma((2,)), dma((2, dim // CHUNK)), dma(()), dma((2, dim // CHUNK)), dma((2,)), dma((2,)),
         ],
         compiler_params=pltpu.CompilerParams(
             collective_id=0, has_side_effects=True, vmem_limit_bytes=VMEM_LIMIT),
@@ -549,45 +535,54 @@
     )(x_a, h_b, attn_b, r_a, r_b, g_a, g_b, w_qkv, w_o, w_gate, w_up, w_down)
 
 
-def hand_on_kernel(n, *refs):
-    ins, outs, bufs = refs[:n], refs[n:2 * n], refs[2 * n:3 * n]
-    in_sem, out_sem = refs[3 * n:]
-    parts = []
-    for a in range(n):
-        for p in range(ins[a].shape[1] // 1024):
-            parts.append((a, slice(1024 * p, 1024 * (p + 1)), len(parts)))
-    gets = [pltpu.make_async_copy(ins[a].at[:, c], bufs[a].at[:, c], in_sem.at[i]) for a, c, i in parts]
-    puts = [pltpu.make_async_copy(bufs[a].at[:, c], outs[a].at[:, c], out_sem.at[i]) for a, c, i in parts]
-    for g in gets:
+def hand_on_kernel(mine, back, out_a, out_b, qkv, to_a, to_b, to_qkv, buf_a, buf_b, buf_qkv, sums, in_sem, out_sem, sum_sem):
+    width = out_b.shape[1]
+    last = slice(width - CHUNK, width)
+    moves = [(out_b, buf_b, to_b, last)]
+    for src, buf, dst in ((qkv, buf_qkv, to_qkv), (out_a, buf_a, to_a), (out_b, buf_b, to_b)):
+        for lo in range(0, src.shape[1], 2 * CHUNK):
+            hi = min(lo + 2 * CHUNK, src.shape[1] - (CHUNK if src is out_b else 0))
+            moves.append((src, buf, dst, slice(lo, hi)))
+    parts = [pltpu.make_async_copy(mine.at[1, :, last], sums.at[0], sum_sem.at[0]),
+             pltpu.make_async_copy(back.at[1, :, last], sums.at[1], sum_sem.at[1])]
+    gets = [pltpu.make_async_copy(s.at[:, c], b.at[:, c], in_sem.at[i]) for i, (s, b, _, c) in enumerate(moves)]
+    puts = [pltpu.make_async_copy(b.at[:, c], d.at[:, c], out_sem.at[i]) for i, (_, b, d, c) in enumerate(moves)]
+    for g in parts + gets:
         g.start()
-    for g, p in zip(gets, puts):
+    for i, (g, p) in enumerate(zip(gets, puts)):
         g.wait()
+        if i == 0:
+            for c in parts:
+                c.wait()
+            total = buf_b[:, last].astype(F32) + (sums[0] + sums[1])
+            buf_b[:, last] = total.astype(BF16)
         p.start()
     for p in puts:
         p.wait()
 
 
-def hand_on(*arrays):
-    n = len(arrays)
-    count = sum(a.shape[1] // 1024 for a in arrays)
+def hand_on(mine, back, *arrays):
+    tok = mine.shape[1]
+    count = 1 + sum(a.shape[1] // (2 * CHUNK) for a in arrays)
     hbm = pl.BlockSpec(memory_space=pl.ANY)
+    dma = pltpu.SemaphoreType.DMA
     return pl.pallas_call(
-        functools.partial(hand_on_kernel, n),
-        in_specs=[hbm] * n,
-        out_specs=[hbm] * n,
+        hand_on_kernel,
+        in_specs=[hbm] * 5,
+        out_specs=[hbm] * 3,
         out_shape=[jax.ShapeDtypeStruct(a.shape, a.dtype) for a in arrays],
         scratch_shapes=[pltpu.VMEM(a.shape, a.dtype) for a in arrays] + [
-            pltpu.SemaphoreType.DMA((count,)), pltpu.SemaphoreType.DMA((count,))],
+            pltpu.VMEM((2, tok, CHUNK), F32), dma((count,)), dma((count,)), dma((2,))],
         compiler_params=pltpu.CompilerParams(vmem_limit_bytes=VMEM_LIMIT),
         name='hand_on',
-    )(*arrays)
+    )(mine, back, *arrays)
 
 
 def solution(mesh):
     def local_step(x_a, route_a, gate_a, h_b, attn_b, route_b, gate_b, w_qkv, w_o, w_gate, w_up, w_down):
-        _, _, out_a, out_b, qkv_b, _ = moe_layer(
+        mine, back, out_a, out_b, qkv_b = moe_layer(
             x_a, h_b, attn_b, route_a.T, route_b.T, gate_a.T, gate_b.T, w_qkv, w_o, w_gate, w_up, w_down)
-        out_a, out_b, qkv_b = hand_on(out_a, out_b, qkv_b)
+        out_a, out_b, qkv_b = hand_on(mine, back, out_a, out_b, qkv_b)
         return out_a, out_b, qkv_b
 
     row_spec = P(('dp', 'ep'), None)

time: 207 us -> 204 us (0.986)
  Pallas kernels: 206 us -> 202 us
    pallas_call x2, Pallas kernels: 206 us -> 202 us  [the longest x1 197 us: moe_layer(): pl.pallas_call(layer_kernel, in_specs=[hbm] * 12, out_specs=[hbm] * 5, ou...]
where the time goes in v7:
time: 204 us; the launch traced here: 203 us
  Pallas kernels  202 us (99%)
    pallas_call x1, Pallas kernels, moe_layer(): pl.pallas_call(layer_kernel, in_specs=[hbm] * 12, out_specs=[hbm] * 5, ou...  197 us
    pallas_call x1, Pallas kernels, hand_on(): pl.pallas_call(hand_on_kernel, in_specs=[hbm] * 5, out_specs=[hbm] * 3, o...  5.31 us

profile of v7, /device:TPU:0, one launch (start us, length us, event | category | flops | bytes accessed | tf_op | source)
XLA Modules:
  0.0 203.3 jit_solution(16571144676783258845)
XLA Ops:
  0.6 197.1 %moe_layer.1 = (f32[2,256,2048]{2,1,0:T(8,128)}, f32[2,256,2048]{2,1,0:T(8,128)}, bf16[256,2048]{1,0:T(8,128)(2,1)}, bf16[256,2048]{1,0:T(8,128)(2,1)}, bf16[256,6144]{1,0:T(8,128)(2,1)}) custom-call(bf16[256,2048]{1,0:T(8,128)(2,1)} %x_hbm.1, bf16[256,2048]{1,0:T(8,128)(2,1)} %h_hbm.1, bf16[256,2048]{1,0:T(8,128)(2,1)} %attn_hbm.1, s32[4,256]{1,0:T(4,128)} %bitcast.4, ...), custom_call_target="tpu_custom_call" | custom-call | flops 83332431872 | bytes 259522560 | tf_op jit(solution)/shard_map/moe_layer/pallas_call | solution.py:504
  197.8 5.3 %hand_on.1 = (bf16[256,2048]{1,0:T(8,128)(2,1)}, bf16[256,2048]{1,0:T(8,128)(2,1)}, bf16[256,6144]{1,0:T(8,128)(2,1)}) custom-call(f32[2,256,2048]{2,1,0:T(8,128)} %get-tuple-element.8.mine, f32[2,256,2048]{2,1,0:T(8,128)} %get-tuple-element.9.back, bf16[256,2048]{1,0:T(8,128)(2,1)} %get-tuple-element.10.out_a, bf16[256,2048]{1,0:T(8,128)(2,1)} %get-tuple-element.11.out_b, ...), custom_call_target="tpu_custom_call" | custom-call | tf_op jit(solution)/shard_map/hand_on/pallas_call | solution.py:569

commit v8 on v7

--- a/solution.py
+++ b/solution.py
@@ -102,9 +102,6 @@
     meta = [(ra_hbm, rv, 0), (rb_hbm, rv, 1), (ga_hbm, gv, 0), (gb_hbm, gv, 1)]
     for i, (src, dst, m) in enumerate(meta):
         loads.append(pltpu.make_async_copy(src, dst.at[0, m], load_sem.at[3 + i]))
-    for c in loads[:2]:
-        c.start()
-    start('o', 0, 0)
     meta_out = []
     for way, who, place in ((0, peer, 2), (1, sib, 1)):
         for i, (src, dst, m) in enumerate(meta):
@@ -113,6 +110,9 @@
                 remote(x_hbm, xv.at[0, 1], row_send.at[0, 1], row_recv.at[0, 1], sib)]
     for c in meta_out + rows_out:
         c.start()
+    for c in loads[:2]:
+        c.start()
+    start('o', 0, 0)
     for c in loads[2:]:
         c.start()
     start('q', 0, 1)
@@ -446,13 +446,13 @@
     dispatch(0, 3, 0, n_first, SLOTS, 0)
     first_hidden()
     lax.fori_loop(1, n_first, gate_up_a, 0)
-    for k in range(4):
+    dispatch(0, 0, n_first, n_both, 2 * SLOTS, 0)
+    forward_b = forward(1)
+    for k in range(1, 4):
         dispatch(0, k, n_first, n_both, 2 * SLOTS, 0)
     rows_out[3].wait_recv()
-    dispatch(1, 0, n_first, n_both, 2 * SLOTS, SLOTS)
-    dispatch(1, 1, n_first, n_both, 2 * SLOTS, SLOTS)
-    forward_b = forward(1)
-    dispatch(1, 2, n_first, n_both, 2 * SLOTS, SLOTS)
+    for k in range(3):
+        dispatch(1, k, n_first, n_both, 2 * SLOTS, SLOTS)
     forward_b.wait_recv()
     dispatch(1, 3, n_first, n_both, 2 * SLOTS, SLOTS)
     lax.fori_loop(0, n_both, gate_up_ab, 0)

time: 204 us -> 202 us (level)
  no operation moved by 1% of the time
where the time goes in v8:
time: 202 us; the launch traced here: 201 us
  Pallas kernels  201 us (100%)
    pallas_call x1, Pallas kernels, moe_layer(): pl.pallas_call(layer_kernel, in_specs=[hbm] * 12, out_specs=[hbm] * 5, ou...  195 us
    pallas_call x1, Pallas kernels, hand_on(): pl.pallas_call(hand_on_kernel, in_specs=[hbm] * 5, out_specs=[hbm] * 3, o...  5.31 us

profile of v8, /device:TPU:0, one launch (start us, length us, event | category | flops | bytes accessed | tf_op | source)
XLA Modules:
  0.0 201.4 jit_solution(18257861679916215600)
XLA Ops:
  0.6 195.3 %moe_layer.1 = (f32[2,256,2048]{2,1,0:T(8,128)}, f32[2,256,2048]{2,1,0:T(8,128)}, bf16[256,2048]{1,0:T(8,128)(2,1)}, bf16[256,2048]{1,0:T(8,128)(2,1)}, bf16[256,6144]{1,0:T(8,128)(2,1)}) custom-call(bf16[256,2048]{1,0:T(8,128)(2,1)} %x_hbm.1, bf16[256,2048]{1,0:T(8,128)(2,1)} %h_hbm.1, bf16[256,2048]{1,0:T(8,128)(2,1)} %attn_hbm.1, s32[4,256]{1,0:T(4,128)} %bitcast.4, ...), custom_call_target="tpu_custom_call" | custom-call | flops 83332431872 | bytes 259522560 | tf_op jit(solution)/shard_map/moe_layer/pallas_call | solution.py:504
  195.9 5.3 %hand_on.1 = (bf16[256,2048]{1,0:T(8,128)(2,1)}, bf16[256,2048]{1,0:T(8,128)(2,1)}, bf16[256,6144]{1,0:T(8,128)(2,1)}) custom-call(f32[2,256,2048]{2,1,0:T(8,128)} %get-tuple-element.8.mine, f32[2,256,2048]{2,1,0:T(8,128)} %get-tuple-element.9.back, bf16[256,2048]{1,0:T(8,128)(2,1)} %get-tuple-element.10.out_a, bf16[256,2048]{1,0:T(8,128)(2,1)} %get-tuple-element.11.out_b, ...), custom_call_target="tpu_custom_call" | custom-call | tf_op jit(solution)/shard_map/hand_on/pallas_call | solution.py:569
